TPU v7x, 16 devices: a whole 2x2x2 slice. The times are simulated.
16 devices in a mesh: dp: 16 (over z, y, x, core).
Axes of the slice: x: 2, y: 2, z: 2, core: 2. Of those that a mesh axis runs over, the one named last changes fastest.
Arguments:
- query: bfloat16 [512, 28, 128], P('dp')
- k_cache: bfloat16 [512, 512, 4, 128], P('dp')
- v_cache: bfloat16 [512, 512, 4, 128], P('dp')
- cache_lens: int32 [512], P('dp')
- dest_slot: int32 [512], replicated
- k_new: bfloat16 [512, 4, 128], P('dp')
- v_new: bfloat16 [512, 4, 128], P('dp')
Outputs:
- output 1: bfloat16 [512, 28, 128], P('dp')
- output 2: bfloat16 [512, 512, 4, 128], P('dp')
- output 3: bfloat16 [512, 512, 4, 128], P('dp')
- output 4: int32 [512], P('dp')
All inputs are finite; a program needn't handle non-finite values.
Results may differ from a plain program's by a relative error of at most 0.001.
Values are sent between devices in bfloat16 or wider.
A program may use at most 1 GiB of HBM per device.

v0:
```python
import functools
import itertools

import jax
import jax.numpy as jnp
import numpy as np
from jax import lax
from jax.experimental import pallas as pl
from jax.experimental.pallas import tpu as pltpu
from jax.sharding import PartitionSpec as P


I32, F32, BF = jnp.int32, jnp.float32, jnp.bfloat16
DEVS, SLOTS, TOTAL = 16, 32, 512
CHIPS, CHIP_SLOTS = 8, 64
DESTS = range(1, CHIPS)
ROWS = 512
HEADS, KV, DIM, GROUP = 28, 4, 128, 7
LANES = 128
BATCHES = (0, 1)
PRE = 6912
POST = 6656
HALF = ROWS // 2
CLASSES = (2224, 2552, 2752, 2984, 3176, 3400, 3592, 4600)
ITERS = 12
FIRST_STEP, SHRINK = 1.5, 15 ** (-1 / 11)
LAST = jnp.iinfo(jnp.int32).max
VMEM_LIMIT = 62914560
TABLES = 40


def make_options():
    found = []
    for b in DESTS:
        dims = [k for k in range(3) if (b >> k) & 1]
        mine = []
        for steps in itertools.combinations(range(3), len(dims)):
            for order in itertools.permutations(dims):
                place, hops = 0, []
                for step, k in zip(steps, order):
                    hops.append((step, place, k))
                    place ^= 1 << k
                mine.append((b, tuple(hops)))
        mine.sort(key=lambda option: (option[1][0][0], option[1][0][2], option[1]))
        found += mine
    return found


OPTIONS = make_options()
N_OPT = len(OPTIONS)
OPT_BASE = [next(o for o in range(N_OPT) if OPTIONS[o][0] == b) for b in DESTS]
OPT_COUNT = [sum(1 for x in OPTIONS if x[0] == b) for b in DESTS]


def make_flows():
    flows = {}
    for step in range(3):
        for k in range(3):
            runs = []
            for o, (_, hops) in enumerate(OPTIONS):
                for h, (st, place, kk) in enumerate(hops):
                    if (st, kk) == (step, k):
                        runs.append((place, o, h))
            runs.sort(key=lambda run: (run[0], run[1]))
            flows[step, k] = runs
    return flows


FLOWS = make_flows()
X_ROW, LO_ROW, S_ROW, C_ROW, META_ROWS = 0, 16, 32, 48, 56
PLACE_LANES = 16
BITS = (1, 2, 4)


def caps_of(rows):
    return rows // 2


def plan_consts():
    hop = np.zeros((LANES, LANES), np.float32)
    group = np.zeros_like(hop)
    before = np.zeros_like(hop)
    dest = np.zeros((CHIPS, LANES), np.float32)
    first = np.zeros_like(dest)
    for o, (b, hops) in enumerate(OPTIONS):
        dest[b, o] = 1
        first[:, o] = o == OPT_BASE[b - 1]
        for step, place, k in hops:
            hop[o, place * PLACE_LANES + step * 3 + k] = 1
        for q, (bb, _) in enumerate(OPTIONS):
            if bb == b:
                group[o, q] = 1
                before[o, q] = o < q
    tri = np.triu(np.ones_like(hop), 1)
    return hop, hop.T.copy(), group, before, dest, first, tri


def plan_kernel(lens_ref, dest_ref, hop_ref, hop_t_ref, group_ref, before_ref, dmat_ref, first_ref, tri_ref, out_ref):
    exact = functools.partial(jnp.dot, preferred_element_type=F32, precision=lax.Precision.HIGHEST)

    def plain(a, b):
        return jnp.dot(a.astype(BF), b.astype(BF), preferred_element_type=F32)

    shape = (CHIPS, LANES)
    row = lax.broadcasted_iota(I32, shape, 0)
    lane = lax.broadcasted_iota(I32, shape, 1)

    lens = lens_ref[...].reshape(CHIPS, 2 * LANES)
    lens = jnp.where(lane < SLOTS, lens[:, :LANES], pltpu.roll(lens[:, LANES:], SLOTS, 1))
    lens = jnp.where(lane < CHIP_SLOTS, lens, 0)
    flat = dest_ref[...]
    turned = pltpu.roll(flat, CHIP_SLOTS, 1)
    to = jnp.concatenate([(turned if c & 1 else flat)[c >> 1:(c >> 1) + 1] for c in range(CHIPS)], axis=0)
    rel = (to >> 6) ^ row
    early = (lens + 1) >> 1
    parts = [early.astype(F32), (lens - early).astype(F32)]

    def top_of(a):
        return jnp.max(jnp.max(a, axis=1, keepdims=True), axis=0, keepdims=True)

    tri = tri_ref[...]
    dmat = dmat_ref[...]
    demand = []
    for beta in range(2):
        mine = [jnp.where(rel == b, parts[beta], 0.0) for b in DESTS]
        earlier = plain(jnp.concatenate(mine, axis=0), tri)
        starts = jnp.zeros(shape, F32)
        total = jnp.zeros(shape, F32)
        for b in DESTS:
            starts = jnp.where(rel == b, earlier[(b - 1) * CHIPS:b * CHIPS], starts)
            total = total + jnp.sum(mine[b - 1], axis=1, keepdims=True) * dmat[b:b + 1]
        demand.append(total)
        at = S_ROW + CHIPS * beta
        out_ref[at:at + CHIPS, :] = starts.astype(I32)

    def flip(a, bit):
        return jnp.where((row & bit) == 0, pltpu.roll(a, CHIPS - bit, 0), pltpu.roll(a, bit, 0))

    def link_loads(x, dot):
        y = dot(x, hop_ref[...])
        for bit in BITS[::-1]:
            y = y + flip(pltpu.roll(y, LANES - PLACE_LANES * bit, 1), bit)
            y = jnp.where(lane < PLACE_LANES * bit, y, 0.0)
        return y

    def path_cost(p):
        y = jnp.where(lane < PLACE_LANES, p, 0.0)
        for bit in BITS:
            y = y + pltpu.roll(flip(y, bit), PLACE_LANES * bit, 1)
        return plain(y, hop_t_ref[...])

    both = demand[0] + demand[1]
    used = jnp.sum(dmat, axis=0, keepdims=True) > 0

    def norm(w):
        w = jnp.where(used, jnp.maximum(w, 1e-6), 0.0)
        return w / jnp.where(used, plain(w, group_ref[...]), 1.0)

    weight = norm(jnp.ones(shape, F32))

    def improve(_, carry):
        weight, best, best_top, size = carry
        loads = link_loads(weight * both, plain)
        top = top_of(loads)
        better = top < best_top
        best = jnp.where(better, weight, best)
        best_top = jnp.where(better, top, best_top)
        price = loads / jnp.maximum(top, 1.0)
        for _ in BITS:
            price = price * price
        return norm(weight * jnp.exp(-size * path_cost(price))), best, best_top, size * SHRINK

    start = (weight, weight, jnp.full((1, 1), 3e38, F32), jnp.full((1, 1), FIRST_STEP, F32))
    best = lax.fori_loop(0, ITERS, improve, start)[1]

    pick = jnp.zeros((1, 1), I32)
    for t in range(2):
        total = demand[t]
        x = jnp.minimum(jnp.floor(best * total * 0.995), total)
        x = x + first_ref[...] * (total - exact(x, group_ref[...]))
        top = top_of(link_loads(x, exact))
        top = jnp.where(top_of(-x) > 0.0, 1e6, top)
        need = jnp.zeros((1, 1), I32)
        for rows in CLASSES:
            need = need + (top > caps_of(rows)).astype(I32)
        pick = jnp.maximum(pick, need)
        at = X_ROW + CHIPS * t
        out_ref[at:at + CHIPS, :] = x.astype(I32)
        at = LO_ROW + CHIPS * t
        out_ref[at:at + CHIPS, :] = exact(x, before_ref[...]).astype(I32)

    from_dev = 2 * row + (lane >> 5)
    to_dev = to >> 5
    crossing = jnp.where(from_dev == to_dev, 0.0, parts[0])
    come = jnp.concatenate([jnp.where(to_dev == d, crossing, 0.0) for d in range(DEVS)], axis=0)
    come = plain(come, jnp.ones((LANES, LANES), F32)).reshape(DEVS, CHIPS, LANES)
    over = top_of(jnp.sum(come, axis=1)) - POST
    for core in range(2):
        leave = jnp.where((lane >> 5) == core, crossing, 0.0)
        over = jnp.maximum(over, top_of(jnp.sum(leave, axis=1, keepdims=True)) - PRE)
    pick = jnp.where(over > 0.0, len(CLASSES), pick)
    out_ref[C_ROW:C_ROW + CHIPS, :] = jnp.broadcast_to(pick, shape)


def make_plan(lens_all, dest_slot):
    return pl.pallas_call(
        plan_kernel,
        out_shape=jax.ShapeDtypeStruct((META_ROWS, LANES), I32),
        name='plan',
    )(lens_all, dest_slot.reshape(KV, LANES), *plan_consts())


def gather_kernel(x_ref, out_ref, send_sem, recv_sem):
    me = lax.axis_index('dp')
    barrier = pltpu.get_barrier_semaphore()
    for r in range(1, DEVS):
        pl.semaphore_signal(barrier, inc=1, device_id=(lax.rem(me + r, DEVS),), device_id_type=pl.DeviceIdType.MESH)
    pl.semaphore_wait(barrier, DEVS - 1)
    copies = []
    for r in range(1, DEVS):
        copies.append(pltpu.make_async_remote_copy(
            src_ref=x_ref, dst_ref=out_ref.at[me], send_sem=send_sem.at[r], recv_sem=recv_sem.at[r],
            device_id=(lax.rem(me + r, DEVS),), device_id_type=pl.DeviceIdType.MESH))
        copies[-1].start()
    out_ref[me] = x_ref[...]
    for copy in copies:
        copy.wait()


def gather_lens(my_lens):
    row = jnp.pad(my_lens, (0, LANES - SLOTS)).reshape(1, LANES)
    return pl.pallas_call(
        gather_kernel,
        out_shape=jax.ShapeDtypeStruct((DEVS, 1, LANES), I32),
        in_specs=[VMEM], out_specs=VMEM,
        scratch_shapes=[pltpu.SemaphoreType.DMA((DEVS,))] * 2,
        compiler_params=pltpu.CompilerParams(collective_id=0, has_side_effects=True),
        name='gather_lens',
    )(row).reshape(DEVS, LANES)


def length(lens_ref, slot):
    return lens_ref[(slot >> 5) * LANES + (slot & 31)]


def part_of(m, beta):
    early = (m + 1) >> 1
    return (0, early)[beta], (early, m - early)[beta]


def row_copy(src, s0, dst, d0, n, sem):
    return pltpu.make_async_copy(src.at[pl.ds(s0, n)], dst.at[pl.ds(d0, n)], sem)


def drain(ref, n, sem):
    @pl.when(n > 0)
    def _():
        row_copy(ref, 0, ref, 0, n, sem).wait()


def flush(stage, s0, out, n, sem):
    @pl.when(n > 0)
    def _():
        copy = row_copy(stage, s0, out, 0, n, sem)
        copy.start()
        copy.wait()


def start_copy(core, flip, k_ref, v_ref, s0, dst, d0, n, sem):
    for c, ref in enumerate((v_ref, k_ref) if flip else (k_ref, v_ref)):
        @pl.when(core == c)
        def _(ref=ref):
            row_copy(ref, s0, dst, d0, n, sem).start()


SMEM = pl.BlockSpec(memory_space=pltpu.SMEM)
ANY = pl.BlockSpec(memory_space=pltpu.HBM)
VMEM = pl.BlockSpec(memory_space=pltpu.VMEM)


def rows_of(n, dtype=BF):
    return jax.ShapeDtypeStruct((n, KV, DIM), dtype)


def local_call(kernel, **kwargs):
    return pl.pallas_call(
        kernel, compiler_params=pltpu.CompilerParams(vmem_limit_bytes=VMEM_LIMIT), **kwargs)


def pre_kernel(beta, with_src, dev_ref, lens_ref, dest_ref, k_ref, v_ref, out_ref, *rest):
    if with_src:
        src_ref, stage, sem = rest
    else:
        stage, sem = rest
    dev = dev_ref[0]
    core = dev & 1

    def one(i, q):
        start, n = part_of(lens_ref[i], beta)
        moving = (dest_ref[dev * SLOTS + i] >> 5) != dev
        n = jnp.where(moving, n, 0)

        @pl.when(n > 0)
        def _():
            start_copy(core, True, k_ref, v_ref, i * ROWS + start, stage, q, n, sem)

        return q + n

    total = lax.fori_loop(0, SLOTS, one, I32(0))
    if with_src:
        def invert(i, _):
            for u in range(CHIPS):
                at = i * CHIPS + u
                src_ref[dest_ref[at]] = at
            return 0

        lax.fori_loop(0, TOTAL // CHIPS, invert, 0)
    drain(stage, total, sem)
    flush(stage, 0, out_ref, jnp.minimum(total, PRE), sem)


def pre_pack(beta, with_src, dev, lens, dest, k, v):
    out, specs = [rows_of(PRE)], [ANY]
    if with_src:
        out.append(jax.ShapeDtypeStruct((TOTAL,), I32))
        specs.append(SMEM)
    got = local_call(
        functools.partial(pre_kernel, beta, with_src),
        out_shape=out, out_specs=specs, in_specs=[SMEM] * 3 + [ANY] * 2,
        scratch_shapes=[pltpu.VMEM((SLOTS * HALF, KV, DIM), BF), pltpu.SemaphoreType.DMA],
    )(dev, lens, dest, k, v)
    return got if with_src else got[0]


class Table:
    def __init__(self, meta, chip, beta):
        self.meta, self.at = meta, CHIPS * BATCHES[beta]
        self.row = [(self.at + (chip ^ v)) * LANES for v in range(CHIPS)]

    def x(self, v, o):
        return self.meta[X_ROW * LANES + self.row[v] + o]

    def lo(self, v, o):
        return self.meta[LO_ROW * LANES + self.row[v] + o]

    def start(self, slot):
        return self.meta[S_ROW * LANES + (self.at + (slot // CHIP_SLOTS)) * LANES + (slot & 63)]


def pack_kernel(beta, step, cap, dev_ref, meta, lens_ref, dest_ref, k_ref, v_ref, pre_ref, *rest):
    recv = {}
    n_in = 3 * step
    for q in range(n_in):
        recv[q // 3, q % 3] = rest[q]
    outs = rest[n_in:n_in + 3]
    stage, table_lo, table_hi, table_to, sem, sem_out = rest[n_in + 3:]
    dev = dev_ref[0]
    chip, core = dev >> 1, dev & 1
    plan = Table(meta, chip, beta)
    used = []
    count = I32(0)
    for k in range(3):
        where = I32(0)
        spans = {}
        for place, o, _ in FLOWS[step, k]:
            if place == 0:
                b = OPTIONS[o][0]
                n = plan.x(0, o)
                if b not in spans:
                    spans[b] = [plan.lo(0, o), I32(0), where]
                spans[b][1] = spans[b][1] + n
                where = where + n
        for b in DESTS:
            if b in spans:
                lo, n, to = spans[b]
                table_lo[b * 3 + k] = lo
                table_hi[b * 3 + k] = lo + n
                table_to[b * 3 + k] = to - lo + k * cap
            else:
                table_lo[b * 3 + k] = I32(0)
                table_hi[b * 3 + k] = I32(0)
                table_to[b * 3 + k] = I32(0)
        used.append(where)
        count = count + where

    if step > 0:
        came = {}
        for (st, kk), runs in FLOWS.items():
            if st < step:
                at = I32(0)
                for place, o, h in runs:
                    v = place ^ (1 << kk)
                    n = plan.x(v, o)
                    hops = OPTIONS[o][1]
                    if h + 1 < len(hops) and hops[h + 1][0] == step:
                        came[v, o] = (st, kk, at, n)
                    at = at + n
        for k in range(3):
            for place, o, h in FLOWS[step, k]:
                if place == 0:
                    continue
                st, kk, at, n = came[place, o]

                @pl.when(n > 0)
                def _(st=st, kk=kk, at=at, n=n, to=used[k], k=k):
                    row_copy(recv[st, kk], at, stage, to + k * cap, n, sem).start()

                used[k] = used[k] + n
                count = count + n

    def one(i, q):
        slot = chip * 64 + i
        to_slot = dest_ref[slot]
        mine = (i >> 5) == core
        start, n = part_of(length(lens_ref, slot), beta)
        b = chip ^ (to_slot >> 6)

        @pl.when(b > 0)
        def _():
            begin = plan.start(slot)
            for k in range(3):
                lo = jnp.maximum(begin, table_lo[b * 3 + k])
                hi = jnp.minimum(begin + n, table_hi[b * 3 + k])
                size = hi - lo
                to = table_to[b * 3 + k] + lo
                skip = lo - begin

                @pl.when(size > 0)
                def _():
                    home = (i & 31) * ROWS + start + skip

                    @pl.when(mine)
                    def _():
                        start_copy(core, False, k_ref, v_ref, home, stage, to, size, sem)

                    @pl.when(jnp.logical_not(mine))
                    def _():
                        row_copy(pre_ref, q + skip, stage, to, size, sem).start()

        away = jnp.logical_not(mine) & ((to_slot >> 5) != (slot >> 5))
        return q + jnp.where(away, n, 0)

    lax.fori_loop(0, 64, one, I32(0))
    drain(stage, count, sem)
    for k in range(3):
        @pl.when(used[k] > 0)
        def _(k=k):
            row_copy(stage, k * cap, outs[k], 0, used[k], sem_out.at[k]).start()
    for k in range(3):
        @pl.when(used[k] > 0)
        def _(k=k):
            row_copy(stage, k * cap, outs[k], 0, used[k], sem_out.at[k]).wait()


def pack(beta, step, cap, scalars, k, v, pre, recv):
    dev, meta, lens, dest, _ = scalars
    recv = [recv[q // 3, q % 3] for q in range(3 * step)]
    return local_call(
        functools.partial(pack_kernel, beta, step, cap),
        out_shape=[rows_of(cap)] * 3, out_specs=[ANY] * 3,
        in_specs=[SMEM] * 4 + [ANY] * (3 + len(recv)),
        scratch_shapes=[pltpu.VMEM((3 * cap, KV, DIM), BF)] + [pltpu.SMEM((TABLES,), I32)] * 3
        + [pltpu.SemaphoreType.DMA, pltpu.SemaphoreType.DMA((3,))],
    )(dev, meta, lens, dest, k, v, pre, *recv)


def table_kernel(dev_ref, meta, lo_ref, hi_ref, at_ref, buf_ref):
    for beta in BATCHES:
        plan = Table(meta, dev_ref[0] >> 1, beta)
        base = TABLES * beta
        for (st, kk), runs in FLOWS.items():
            at = I32(0)
            for place, o, h in runs:
                v = place ^ (1 << kk)
                n = plan.x(v, o)
                if h + 1 == len(OPTIONS[o][1]):
                    lo = plan.lo(v, o)
                    lo_ref[base + o] = lo
                    hi_ref[base + o] = lo + n
                    at_ref[base + o] = at - lo
                    buf_ref[base + o] = I32(st * 3 + kk)
                at = at + n


def arrivals(dev, meta):
    return local_call(
        table_kernel, out_shape=[jax.ShapeDtypeStruct((2 * TABLES,), I32)] * 4,
        out_specs=[SMEM] * 4, in_specs=[SMEM] * 2)(dev, meta)


def static_lookup(table, index):
    out = I32(table[0])
    for q in range(1, len(table)):
        out = jnp.where(index == q, I32(table[q]), out)
    return out


def from_links(plan, chip, slot, n, tables, base, recv, dst, to, sem):
    table_lo, table_hi, table_at, buf_ref = tables
    b = chip ^ (slot // CHIP_SLOTS)
    begin = plan.start(slot)
    first = static_lookup([0] + OPT_BASE, b)
    count = static_lookup([0] + OPT_COUNT, b)

    def piece(q, _):
        o = first + q
        lo = jnp.maximum(begin, table_lo[base + o])
        hi = jnp.minimum(begin + n, table_hi[base + o])
        size = hi - lo
        at = table_at[base + o] + lo
        put = to + lo - begin

        @pl.when(size > 0)
        def _():
            which = buf_ref[base + o]
            for w in range(9):
                @pl.when(which == w)
                def _(w=w):
                    row_copy(recv[w], at, dst, put, size, sem).start()

        return 0

    lax.fori_loop(0, count, piece, 0)


def post_kernel(beta, other, dev_ref, meta, lens_ref, dest_ref, src_ref, *rest):
    tables, (k_ref, v_ref, pre_ref, *recv), (out_ref, stage, pre_at, sem) = rest[:4], rest[4:16], rest[16:]
    dev = dev_ref[0]
    chip, core = dev >> 1, dev & 1
    plan = Table(meta, chip, beta)
    sibling = dev ^ 1
    target = sibling if other else dev

    if not other:
        def place(i, q):
            pre_at[i] = q
            slot = sibling * SLOTS + i
            _, n = part_of(length(lens_ref, slot), beta)
            return q + jnp.where((dest_ref[slot] >> 5) != sibling, n, 0)

        lax.fori_loop(0, SLOTS, place, I32(0))

    def one(j, q):
        slot = src_ref[target * SLOTS + j]
        start, n = part_of(length(lens_ref, slot), beta)
        owner = slot >> 5
        n = jnp.where(owner == target, 0, n)
        i = slot & 31

        @pl.when(((owner >> 1) == chip) & (n > 0))
        def _():
            if other:
                start_copy(core, False, k_ref, v_ref, i * ROWS + start, stage, q, n, sem)
            else:
                row_copy(pre_ref, pre_at[i], stage, q, n, sem).start()

        @pl.when((owner >> 1) != chip)
        def _():
            from_links(plan, chip, slot, n, tables, TABLES * beta, recv, stage, q, sem)

        return q + n

    total = lax.fori_loop(0, SLOTS, one, I32(0))
    drain(stage, total, sem)
    flush(stage, 0, out_ref, total, sem)


def post_pack(beta, other, scalars, tables, k, v, pre, recv):
    recv = [recv[q // 3, q % 3] for q in range(9)]
    return local_call(
        functools.partial(post_kernel, beta, other),
        out_shape=rows_of(POST), out_specs=ANY,
        in_specs=[SMEM] * 9 + [ANY] * 12,
        scratch_shapes=[pltpu.VMEM((POST, KV, DIM), BF), pltpu.SMEM((SLOTS,), I32), pltpu.SemaphoreType.DMA],
    )(*scalars, *tables, k, v, pre, *recv)


ZEROS = 480


def zeros_kernel(dev_ref, lens_ref, src_ref, q_ref, ko_ref, vo_ref, lens_out, q_out, zeros, sem):
    dev = dev_ref[0]

    def clear(t, _):
        zeros[pl.ds(t * SLOTS, SLOTS)] = jnp.zeros((SLOTS, KV, DIM), BF)
        return 0

    lax.fori_loop(0, ZEROS // SLOTS, clear, 0)

    def each(wait, j, _):
        m = length(lens_ref, src_ref[dev * SLOTS + j])
        n = ROWS - 1 - m
        if not wait:
            lens_out[j] = m + 1

        @pl.when(n > 0)
        def _():
            for q, out in enumerate((ko_ref, vo_ref)):
                copy = row_copy(zeros, 0, out, j * ROWS + m + 1, n, sem.at[q, j])
                copy.wait() if wait else copy.start()

        return 0

    lax.fori_loop(0, SLOTS, functools.partial(each, False), 0)
    q_out[...] = q_ref[...]
    lax.fori_loop(0, SLOTS, functools.partial(each, True), 0)


def zero_tails(dev, lens, src, query):
    return local_call(
        zeros_kernel,
        out_shape=[rows_of(SLOTS * ROWS)] * 2 + [jax.ShapeDtypeStruct((SLOTS,), I32),
                                               jax.ShapeDtypeStruct(query.shape, BF)],
        out_specs=[ANY, ANY, SMEM, VMEM], in_specs=[SMEM] * 3 + [VMEM],
        scratch_shapes=[pltpu.VMEM((ZEROS, KV, DIM), BF), pltpu.SemaphoreType.DMA((2, SLOTS))],
    )(dev, lens, src, query)


N_BUF, AHEAD, UNROLL = 12, 8, 2


def finish_kernel(dev_ref, lens_ref, src_ref, k_ref, v_ref, *rest):
    land, post = rest[0:2], rest[2:4]
    q_ref, kn_ref, vn_ref, _, _, attn_ref, ko_ref, vo_ref, bufs, cols, moved_at, sem_in, sem_out = rest[4:]
    dev = dev_ref[0]
    core = dev & 1

    def source(j):
        slot = src_ref[dev * SLOTS + j]
        return slot, length(lens_ref, slot)

    def place(j, at):
        slot, m = source(j)
        after = []
        for beta in BATCHES:
            moved_at[SLOTS * beta + j] = at[beta]
            after.append(at[beta] + jnp.where((slot >> 5) != dev, part_of(m, beta)[1], 0))
        return tuple(after)

    lax.fori_loop(0, SLOTS, place, (I32(0), I32(0)))

    def fetch(j):
        slot, m = source(j)
        buf = lax.rem(j, N_BUF)

        @pl.when((slot >> 5) == dev)
        def _():
            home = (slot & 31) * ROWS
            row_copy(k_ref, home, bufs.at[0, buf], 0, m, sem_in.at[0, buf]).start()
            row_copy(v_ref, home, bufs.at[1, buf], 0, m, sem_in.at[1, buf]).start()

        @pl.when((slot >> 5) != dev)
        def _():
            for beta in BATCHES:
                start, n = part_of(m, beta)
                at = moved_at[SLOTS * beta + j]
                for ref, q in ((land[beta], core), (post[beta], 1 - core)):
                    row_copy(ref, at, bufs.at[q, buf], start, n, sem_in.at[q, buf]).start()

    def emit(j, wait):
        _, m = source(j)
        buf = lax.rem(j, N_BUF)
        for q, out in enumerate((ko_ref, vo_ref)):
            copy = row_copy(bufs.at[q, buf], 0, out, j * ROWS, m + 1, sem_out.at[q, buf])
            copy.wait() if wait else copy.start()

    def clear(t, _):
        bufs[1, t // KV, pl.ds((t % KV) * DIM, DIM)] = jnp.zeros((DIM, KV, DIM), BF)
        return 0

    lax.fori_loop(0, KV * N_BUF, clear, 0)

    def begin(j, _):
        fetch(j)
        return 0

    lax.fori_loop(0, AHEAD, begin, 0)
    head = lax.broadcasted_iota(I32, (HEADS, LANES), 0) // GROUP
    col = lax.broadcasted_iota(I32, (HEADS, LANES), 1)
    mine = jnp.where(head == (col & (KV - 1)), col, LAST // 2)

    def number(t, _):
        cols[:, pl.ds(pl.multiple_of(t * LANES, LANES), LANES)] = mine + t * LANES
        return 0

    lax.fori_loop(0, KV * ROWS // LANES, number, 0)

    def some(jj, _):
        def prefetch(u, _):
            ahead = UNROLL * jj + u + AHEAD

            @pl.when(ahead < SLOTS)
            def _():
                @pl.when(ahead >= N_BUF)
                def _():
                    emit(ahead - N_BUF, True)

                fetch(ahead)

            return 0

        lax.fori_loop(0, UNROLL, prefetch, 0)

        def ready(u, _):
            j = UNROLL * jj + u
            _, m = source(j)
            buf = lax.rem(j, N_BUF)
            for q, new in enumerate((kn_ref, vn_ref)):
                row_copy(k_ref, 0, bufs.at[q, buf], 0, m, sem_in.at[q, buf]).wait()
                bufs[q, buf, m] = new[j]
            emit(j, False)
            return 0

        lax.fori_loop(0, UNROLL, ready, 0)
        scores = []
        for u in range(UNROLL):
            j = UNROLL * jj + u
            kk = bufs[0, lax.rem(j, N_BUF)].reshape(KV * ROWS, DIM)
            s = lax.dot_general(q_ref[j], kk, (((1,), (1,)), ((), ())), preferred_element_type=F32)
            scores.append(jnp.where(cols[...] < KV * (source(j)[1] + 1), s * (DIM ** -0.5), -1e30))
        for u, s in enumerate(scores):
            j = UNROLL * jj + u
            p = jnp.exp(s - jnp.max(s, axis=1, keepdims=True))
            total = jnp.sum(p, axis=1, keepdims=True)
            vv = bufs[1, lax.rem(j, N_BUF)].reshape(KV * ROWS, DIM)
            acc = jnp.dot(p.astype(BF), vv, preferred_element_type=F32)
            attn_ref[j] = (acc / total).astype(BF)
        return 0

    lax.fori_loop(0, SLOTS // UNROLL, some, 0)

    def wait_out(j, _):
        emit(j, True)
        return 0

    lax.fori_loop(SLOTS - N_BUF, SLOTS, wait_out, 0)


def finish(scalars, k, v, land, post, query, k_new, v_new, outs):
    in_specs = [SMEM] * 3 + [ANY] * 6 + [VMEM] * 3
    dev, _, lens, _, src = scalars
    attn, ko, vo = local_call(
        finish_kernel,
        out_shape=[jax.ShapeDtypeStruct((SLOTS, HEADS, DIM), BF)] + [rows_of(SLOTS * ROWS)] * 2,
        out_specs=[VMEM, ANY, ANY], in_specs=in_specs + [ANY] * 2,
        input_output_aliases={len(in_specs): 1, len(in_specs) + 1: 2},
        scratch_shapes=[pltpu.VMEM((2, N_BUF, ROWS, KV, DIM), BF), pltpu.VMEM((HEADS, KV * ROWS), I32),
                        pltpu.SMEM((2 * SLOTS,), I32)] + [pltpu.SemaphoreType.DMA((2, N_BUF))] * 2,
    )(dev, lens, src, k, v, *land, *post, query, k_new, v_new, *outs)
    return attn, ko, vo


def swap(x, mask):
    return lax.ppermute(x, 'dp', [(i, i ^ mask) for i in range(DEVS)])


def after(x, *others):
    return lax.optimization_barrier((x, *others))[0]


def routed(rows, scalars, k, v, pre0, my_lens, query):
    dev, meta, lens, dest, src = scalars
    cap = caps_of(rows)
    recv, pre = [{}, {}], [pre0, None]
    turn = dev
    for step in range(3):
        for beta in BATCHES:
            if step == 0 and beta == 1:
                pre_send = pre_pack(1, False, turn, my_lens, dest, k, v)
                pre[1] = swap(pre_send, 1)
                ko, vo, lens_out, query = zero_tails(after(dev, pre_send), lens, src, query)
                tables = arrivals(after(dev, lens_out), meta)
                turn = after(dev, tables[0])
            sends = pack(beta, step, cap, (turn, *scalars[1:]), k, v, pre[beta], recv[beta])
            turn = after(dev, sends[0])
            for dim in range(3):
                recv[beta][step, dim] = swap(sends[dim], 2 << dim)
    land, post = [], []
    for beta in BATCHES:
        packed = post_pack(beta, True, (turn, *scalars[1:]), tables, k, v, pre[beta], recv[beta])
        turn = after(dev, packed)
        post.append(swap(packed, 1))
        land.append(post_pack(beta, False, (turn, *scalars[1:]), tables, k, v, pre[beta], recv[beta]))
        turn = after(dev, land[-1])
    return *land, *post, ko, vo, query, lens_out


def take_kernel(owner_ref, dev_ref, src_ref, kh, vh, _, __, ka, va, stage, sem):
    def one(j, _):
        slot = src_ref[dev_ref[0] * SLOTS + j]

        @pl.when((slot >> 5) == owner_ref[0])
        def _():
            for held, out in ((kh, ka), (vh, va)):
                row_copy(held, (slot & 31) * ROWS, stage, 0, ROWS, sem).start()
                row_copy(held, (slot & 31) * ROWS, stage, 0, ROWS, sem).wait()
                row_copy(stage, 0, out, j * ROWS, ROWS, sem).start()
                row_copy(stage, 0, out, j * ROWS, ROWS, sem).wait()

        return 0

    lax.fori_loop(0, SLOTS, one, 0)


def ring_move(dev, src, k, v):
    shift = [(i, (i + 1) % DEVS) for i in range(DEVS)]

    def turn(r, carry):
        owner = (dev - r) % DEVS
        ka, va = local_call(
            take_kernel, out_shape=[rows_of(SLOTS * ROWS)] * 2, out_specs=[ANY] * 2,
            in_specs=[SMEM] * 3 + [ANY] * 4, input_output_aliases={5: 0, 6: 1},
            scratch_shapes=[pltpu.VMEM((ROWS, KV, DIM), BF), pltpu.SemaphoreType.DMA],
        )(owner, dev, src, *carry)
        return *[lax.ppermute(x, 'dp', shift) for x in carry[:2]], ka, va

    first = turn(0, (k, v, jnp.zeros_like(k), jnp.zeros_like(v)))
    return lax.fori_loop(1, DEVS, turn, first)[2:]


def solution(mesh):
    def local(query, k_cache, v_cache, cache_lens, dest_slot, k_new, v_new):
        dev = lax.axis_index('dp').reshape(1).astype(I32)
        flat, full = (SLOTS * ROWS, KV, DIM), (SLOTS, ROWS, KV, DIM)
        k, v = k_cache.reshape(flat), v_cache.reshape(flat)
        lens = gather_lens(cache_lens)
        pre_send, src = pre_pack(0, True, after(dev, lens), cache_lens, dest_slot, k, v)
        pre0 = swap(pre_send, 1)
        plan = make_plan(lens, dest_slot)
        scalars = (dev, plan.reshape(-1), lens.reshape(-1), dest_slot, src)

        def route(rows, args):
            return routed(rows, *args)

        def fast(args):
            scalars, k, v, pre0, my_lens, query, k_new, v_new, pick = args
            branches = [functools.partial(route, rows) for rows in CLASSES]
            *came, ko, vo, query, lens_out = lax.switch(pick, branches, (scalars, k, v, pre0, my_lens, query))
            return *finish(scalars, k, v, came[:2], came[2:], query, k_new, v_new, (ko, vo)), lens_out

        def slow(args):
            (dev, meta, lens, dest, src), k, v, _, _, query, k_new, v_new, _ = args
            ka, va = ring_move(dev, src, k, v)
            mine = length(lens, lax.dynamic_slice(src, (dev[0] * SLOTS,), (SLOTS,)))
            mine = jnp.tile(jnp.pad(mine, (0, LANES - SLOTS)), DEVS)
            here = (dev, meta, mine, dest, jnp.arange(TOTAL, dtype=I32))
            none = [jnp.zeros((CHIPS, KV, DIM), BF)] * 2
            *outs, lens_out, query = zero_tails(dev, mine, here[-1], query)
            return *finish(here, ka, va, none, none, query, k_new, v_new, outs), lens_out

        pick = plan[C_ROW, 0]
        attn, ko, vo, lens_out = lax.cond(
            pick < len(CLASSES), fast, slow, (scalars, k, v, pre0, cache_lens, query, k_new, v_new, pick))
        return attn, ko.reshape(full), vo.reshape(full), lens_out

    row_spec = P('dp')
    return jax.shard_map(local, mesh=mesh, in_specs=(row_spec, row_spec, row_spec, row_spec, P(), row_spec, row_spec), out_specs=(row_spec, row_spec, row_spec, row_spec), check_vma=False)
```

profile of v0, /device:TPU:0, one launch (start us, length us, event | category | flops | bytes accessed | tf_op | source)
XLA Modules:
  0.0 240.1 jit_solution(852109955666497294)
XLA Ops:
  1.8 8.3 %gather_lens.1 = s32[16,1,128]{2,1,0:T(1,128)S(1)} custom-call(s32[1,128]{1,0:T(1,128)} %pad_bitcast_fusion.x_ref), custom_call_target="tpu_custom_call" | custom-call | tf_op jit(solution)/shard_map/gather_lens/pallas_call | solution.py:232
  10.1 6.5 %shard_map.165 = (bf16[6912,4,128]{2,1,0:T(4,128)(2,1)}, s32[512]{0:T(512)S(1)}) custom-call(s32[1]{0:T(128)} %bitcast.7.dev_ref, s32[32]{0:T(128)} %lens_ref.1, s32[512]{0:T(512)} %dest_ref.1, bf16[16384,4,128]{2,1,0:T(4,128)(2,1)} %bitcast.17, bf16[16384,4,128]{2,1,0:T(4,128)(2,1)} %bitcast.20), custom_call_target="tpu_custom_call" | custom-call | tf_op jit(solution)/shard_map/pallas_call | solution.py:327
  16.7 12.9 %plan.1 = s32[56,128]{1,0:T(8,128)S(1)} custom-call(s32[16,128]{1,0:T(8,128)S(1)} %bitcast.31, s32[4,128]{1,0:T(4,128)S(1)} %bitcast.36, f32[128,128]{1,0:T(8,128)} %constant.119.clone.hop_ref, f32[128,128]{1,0:T(8,128)} %constant.120.clone.hop_t_ref, f32[128,128]{1,0:T(8,128)} %constant.121.clone.group_ref, f32[128,128]{1,0:T(8,128)} %constant.122.clone.before_ref, ...), custom_call_target="tpu_custom_call" | custom-call | tf_op jit(solution)/shard_map/plan/pallas_call | solution.py:206
  30.9 207.5 %conditional.2 = (bf16[32,28,128]{2,1,0:T(8,128)(2,1)}, bf16[16384,4,128]{2,1,0:T(4,128)(2,1)}, bf16[16384,4,128]{2,1,0:T(4,128)(2,1)}, s32[32]{0:T(128)}) conditional(s32[]{:T(128)} %convert_element_type.3, (s32[]{:T(128)}, s32[512]{0:T(512)S(1)}, s32[2048]{0:T(1024)S(1)}, bf16[16384,4,128]{2,1,0:T(4,128)(2,1)}, bf16[16384,4,128]{2,1,0:T(4,128)(2,1)}, ...), branch_computations={%region_0.3_spmd, %region_3.12_spmd} | conditional | flops 1277 | bytes 369846944 | solution.py:852
  33.3 183.0 %conditional = (bf16[6656,4,128]{2,1,0:T(4,128)(2,1)}, bf16[6656,4,128]{2,1,0:T(4,128)(2,1)}, bf16[6656,4,128]{2,1,0:T(4,128)(2,1)}, bf16[6656,4,128]{2,1,0:T(4,...) conditional(s32[]{:T(128)} %clamp.2, (s32[1]{0:T(128)}, ...), branch_computations={%region_4.4_spmd, %region_5.5_spmd, %region_6.6_spmd, %region_7.7_... | conditional | bytes 280798720 | solution.py:838
  33.4 5.8 %branch_0_fun.19 = (bf16[1112,4,128]{2,1,0:T(4,128)(2,1)}, bf16[1112,4,128]{2,1,0:T(4,128)(2,1)}, bf16[1112,4,128]{2,1,0:T(4,128)(2,1)}) custom-call(s32[1]{0:T(128)} %get-tuple-element.441.dev_ref, s32[7168]{0:T(1024)} %get-tuple-element.398.meta, s32[2048]{0:T(1024)S(1)} %get-tuple-element.399.lens_ref, s32[512]{0:T(512)} %get-tuple-element.400.dest_ref, ...), custom_call_target="tpu_custom_call" | custom-call | tf_op jit(solution)/shard_map/cond/branch_1_fun/cond/branch_0_fun/pallas_call | solution.py:458
  39.2 5.5 %branch_0_fun.20 = bf16[6912,4,128]{2,1,0:T(4,128)(2,1)} custom-call(s32[1]{0:T(128)} %get-tuple-element.441.dev_ref, s32[32]{0:T(128)S(1)} %copy-done.67, s32[512]{0:T(512)S(1)} %copy-done.26, bf16[16384,4,128]{2,1,0:T(4,128)(2,1)} %get-tuple-element.401.k_ref.rest_4_, bf16[16384,4,128]{2,1,0:T(4,128)(2,1)} %get-tuple-element.402.v_ref.rest_5_), custom_call_target="tpu_custom_call" | custom-call | tf_op jit(solution)/shard_map/cond/branch_1_fun/cond/branch_0_fun/pallas_call | solution.py:327
  44.8 2.6 %collective-permute-start.1 = (bf16[1112,4,128]{2,1,0:T(4,128)(2,1)}, bf16[1112,4,128]{2,1,0:T(4,128)(2,1)S(1)}, u32[]{:S(2)}, u32[]{:S(2)}) collective-permute-start(bf16[1112,4,128]{2,1,0:T(4,128)(2,1)} %get-tuple-element.404), channel_id=1, source_target_pairs={{0,2},{1,3},{2,0},{3,1},{4,6},{5,7},{6,4},{7,5},{8,10},{9,11},{10,... | collective-permute-start | bytes 3416072 | tf_op jit(solution)/shard_map/cond/branch_1_fun/cond/branch_0_fun/ppermute | solution.py:754
  48.6 6.3 %branch_0_fun.21 = (bf16[16384,4,128]{2,1,0:T(4,128)(2,1)}, bf16[16384,4,128]{2,1,0:T(4,128)(2,1)}, s32[32]{0:T(128)}, bf16[32,28,128]{2,1,0:T(8,128)(2,1)S(1)}) custom-call(s32[1]{0:T(128)} %get-tuple-element.441.dev_ref, s32[2048]{0:T(1024)S(1)} %get-tuple-element.399.lens_ref, s32[512]{0:T(512)S(1)} %get-tuple-element.408.src_ref, ...), custom_call_target="tpu_custom_call" | custom-call | tf_op jit(solution)/shard_map/cond/branch_1_fun/cond/branch_0_fun/pallas_call | solution.py:610
  54.9 1.8 branch_0_fun.22
  56.8 5.6 %branch_0_fun.23 = (bf16[1112,4,128]{2,1,0:T(4,128)(2,1)}, bf16[1112,4,128]{2,1,0:T(4,128)(2,1)}, bf16[1112,4,128]{2,1,0:T(4,128)(2,1)}) custom-call(s32[1]{0:T(128)} %get-tuple-element.441.dev_ref, s32[7168]{0:T(1024)S(1)} %copy-done.1, s32[2048]{0:T(1024)S(1)} %get-tuple-element.399.lens_ref, s32[512]{0:T(512)S(1)} %copy-done.26, ...), custom_call_target="tpu_custom_call" | custom-call | tf_op jit(solution)/shard_map/cond/branch_1_fun/cond/branch_0_fun/pallas_call | solution.py:458
  62.4 3.9 %collective-permute-start.4 = (bf16[1112,4,128]{2,1,0:T(4,128)(2,1)}, bf16[1112,4,128]{2,1,0:T(4,128)(2,1)S(1)}, u32[]{:S(2)}, u32[]{:S(2)}) collective-permute-start(bf16[1112,4,128]{2,1,0:T(4,128)(2,1)} %get-tuple-element.414), channel_id=1, source_target_pairs={{0,2},{1,3},{2,0},{3,1},{4,6},{5,7},{6,4},{7,5},{8,10},{9,11},{10,... | collective-permute-start | bytes 3416072 | tf_op jit(solution)/shard_map/cond/branch_1_fun/cond/branch_0_fun/ppermute | solution.py:754
  66.3 7.2 %collective-permute-done.1.rest_0_.rest_7_ = bf16[1112,4,128]{2,1,0:T(4,128)(2,1)S(1)} collective-permute-done((bf16[1112,4,128]{2,1,0:T(4,128)(2,1)}, bf16[1112,4,128]{2,1,0:T(4,128)(2,1)S(1)}, u32[]{:S(2)}, u32[]{:S(2)}) %collective-permute-start.1) | collective-permute-done | bytes 1138720 | tf_op jit(solution)/shard_map/cond/branch_1_fun/cond/branch_0_fun/ppermute | solution.py:754
  75.7 6.0 %branch_0_fun.24 = (bf16[1112,4,128]{2,1,0:T(4,128)(2,1)}, bf16[1112,4,128]{2,1,0:T(4,128)(2,1)}, bf16[1112,4,128]{2,1,0:T(4,128)(2,1)}) custom-call(s32[1]{0:T(128)} %get-tuple-element.441.dev_ref, s32[7168]{0:T(1024)S(1)} %copy-done.1, s32[2048]{0:T(1024)S(1)} %get-tuple-element.399.lens_ref, s32[512]{0:T(512)S(1)} %copy-done.26, ...), custom_call_target="tpu_custom_call" | custom-call | tf_op jit(solution)/shard_map/cond/branch_1_fun/cond/branch_0_fun/pallas_call | solution.py:458
  83.2 14.7 %collective-permute-done.4.rest_0_.rest_7_ = bf16[1112,4,128]{2,1,0:T(4,128)(2,1)S(1)} collective-permute-done((bf16[1112,4,128]{2,1,0:T(4,128)(2,1)}, bf16[1112,4,128]{2,1,0:T(4,128)(2,1)S(1)}, u32[]{:S(2)}, u32[]{:S(2)}) %collective-permute-start.4) | collective-permute-done | bytes 1138720 | tf_op jit(solution)/shard_map/cond/branch_1_fun/cond/branch_0_fun/ppermute | solution.py:754
  100.9 6.1 %branch_0_fun.25 = (bf16[1112,4,128]{2,1,0:T(4,128)(2,1)}, bf16[1112,4,128]{2,1,0:T(4,128)(2,1)}, bf16[1112,4,128]{2,1,0:T(4,128)(2,1)}) custom-call(s32[1]{0:T(128)} %get-tuple-element.441.dev_ref, s32[7168]{0:T(1024)S(1)} %copy-done.1, s32[2048]{0:T(1024)S(1)} %get-tuple-element.399.lens_ref, s32[512]{0:T(512)S(1)} %copy-done.26, ...), custom_call_target="tpu_custom_call" | custom-call | tf_op jit(solution)/shard_map/cond/branch_1_fun/cond/branch_0_fun/pallas_call | solution.py:458
  107.0 1.7 collective-permute-start.10
  108.6 13.7 %collective-permute-done.7.rest_3_.rest_10_ = bf16[1112,4,128]{2,1,0:T(4,128)(2,1)S(1)} collective-permute-done((bf16[1112,4,128]{2,1,0:T(4,128)(2,1)}, bf16[1112,4,128]{2,1,0:T(4,128)(2,1)S(1)}, u32[]{:S(2)}, u32[]{:S(2)}) %collective-permute-start.7) | collective-permute-done | bytes 1138720 | tf_op jit(solution)/shard_map/cond/branch_1_fun/cond/branch_0_fun/ppermute | solution.py:754
  124.5 6.3 %branch_0_fun.26 = (bf16[1112,4,128]{2,1,0:T(4,128)(2,1)}, bf16[1112,4,128]{2,1,0:T(4,128)(2,1)}, bf16[1112,4,128]{2,1,0:T(4,128)(2,1)}) custom-call(s32[1]{0:T(128)} %get-tuple-element.441.dev_ref, s32[7168]{0:T(1024)S(1)} %copy-done.1, s32[2048]{0:T(1024)S(1)} %get-tuple-element.399.lens_ref, s32[512]{0:T(512)S(1)} %copy-done.26, ...), custom_call_target="tpu_custom_call" | custom-call | tf_op jit(solution)/shard_map/cond/branch_1_fun/cond/branch_0_fun/pallas_call | solution.py:458
  130.8 1.8 collective-permute-start.13
  132.6 14.1 %collective-permute-done.10.rest_3_.rest_10_ = bf16[1112,4,128]{2,1,0:T(4,128)(2,1)S(1)} collective-permute-done((bf16[1112,4,128]{2,1,0:T(4,128)(2,1)}, bf16[1112,4,128]{2,1,0:T(4,128)(2,1)S(1)}, u32[]{:S(2)}, u32[]{:S(2)}) %collective-permute-start.10) | collective-permute-done | bytes 1138720 | tf_op jit(solution)/shard_map/cond/branch_1_fun/cond/branch_0_fun/ppermute | solution.py:754
  149.8 6.3 %branch_0_fun.27 = (bf16[1112,4,128]{2,1,0:T(4,128)(2,1)}, bf16[1112,4,128]{2,1,0:T(4,128)(2,1)}, bf16[1112,4,128]{2,1,0:T(4,128)(2,1)}) custom-call(s32[1]{0:T(128)} %get-tuple-element.441.dev_ref, s32[7168]{0:T(1024)S(1)} %copy-done.1, s32[2048]{0:T(1024)S(1)} %get-tuple-element.399.lens_ref, s32[512]{0:T(512)S(1)} %copy-done.26, ...), custom_call_target="tpu_custom_call" | custom-call | tf_op jit(solution)/shard_map/cond/branch_1_fun/cond/branch_0_fun/pallas_call | solution.py:458
  157.7 13.5 %collective-permute-done.13.rest_13_ = bf16[1112,4,128]{2,1,0:T(4,128)(2,1)S(1)} collective-permute-done((bf16[1112,4,128]{2,1,0:T(4,128)(2,1)}, bf16[1112,4,128]{2,1,0:T(4,128)(2,1)S(1)}, u32[]{:S(2)}, u32[]{:S(2)}) %collective-permute-start.13) | collective-permute-done | bytes 1138720 | tf_op jit(solution)/shard_map/cond/branch_1_fun/cond/branch_0_fun/ppermute | solution.py:754
  173.3 5.0 %branch_0_fun.28 = bf16[6656,4,128]{2,1,0:T(4,128)(2,1)} custom-call(s32[1]{0:T(128)} %get-tuple-element.441.dev_ref, s32[7168]{0:T(1024)S(1)} %copy-done.1, s32[2048]{0:T(1024)S(1)} %get-tuple-element.399.lens_ref, s32[512]{0:T(512)S(1)} %copy-done.26, s32[512]{0:T(512)S(1)} %get-tuple-element.408.src_ref, s32[80]{0:T(128)} %get-tuple-element.412.rest_0_, ...), custom_call_target="tpu_custom_call" | custom-call | tf_op jit(solution)/shard_map/cond/branch_1_fun/cond/branch_0_fun/pallas_call | solution.py:570
  178.3 2.5 %collective-permute-start.19 = (bf16[6656,4,128]{2,1,0:T(4,128)(2,1)}, bf16[6656,4,128]{2,1,0:T(4,128)(2,1)}, u32[]{:S(2)}, u32[]{:S(2)}) collective-permute-start(bf16[6656,4,128]{2,1,0:T(4,128)(2,1)} %branch_0_fun.28), channel_id=1, source_target_pairs={{0,1},{1,0},{2,3},{3,2},{4,5},{5,4},{6,7},{7,6},{8,9},{9,8},{10,11... | collective-permute-start | bytes 20447240 | tf_op jit(solution)/shard_map/cond/branch_1_fun/cond/branch_0_fun/ppermute | solution.py:754
  180.8 9.1 %branch_0_fun.29 = bf16[6656,4,128]{2,1,0:T(4,128)(2,1)} custom-call(s32[1]{0:T(128)} %get-tuple-element.441.dev_ref, s32[7168]{0:T(1024)S(1)} %copy-done.1, s32[2048]{0:T(1024)S(1)} %get-tuple-element.399.lens_ref, s32[512]{0:T(512)S(1)} %copy-done.26, s32[512]{0:T(512)S(1)} %get-tuple-element.408.src_ref, s32[80]{0:T(128)} %get-tuple-element.412.rest_0_, ...), custom_call_target="tpu_custom_call" | custom-call | tf_op jit(solution)/shard_map/cond/branch_1_fun/cond/branch_0_fun/pallas_call | solution.py:570
  189.9 5.0 %collective-permute-done.16.rest_13_ = bf16[1112,4,128]{2,1,0:T(4,128)(2,1)S(1)} collective-permute-done((bf16[1112,4,128]{2,1,0:T(4,128)(2,1)}, bf16[1112,4,128]{2,1,0:T(4,128)(2,1)S(1)}, u32[]{:S(2)}, u32[]{:S(2)}) %collective-permute-start.16) | collective-permute-done | bytes 1138720 | tf_op jit(solution)/shard_map/cond/branch_1_fun/cond/branch_0_fun/ppermute | solution.py:754
  197.6 5.2 %branch_0_fun.30 = bf16[6656,4,128]{2,1,0:T(4,128)(2,1)} custom-call(s32[1]{0:T(128)} %get-tuple-element.441.dev_ref, s32[7168]{0:T(1024)S(1)} %copy-done.1, s32[2048]{0:T(1024)S(1)} %get-tuple-element.399.lens_ref, s32[512]{0:T(512)S(1)} %copy-done.26, s32[512]{0:T(512)S(1)} %get-tuple-element.408.src_ref, s32[80]{0:T(128)} %get-tuple-element.412.rest_0_, ...), custom_call_target="tpu_custom_call" | custom-call | tf_op jit(solution)/shard_map/cond/branch_1_fun/cond/branch_0_fun/pallas_call | solution.py:570
  202.8 2.7 %collective-permute-start.20 = (bf16[6656,4,128]{2,1,0:T(4,128)(2,1)}, bf16[6656,4,128]{2,1,0:T(4,128)(2,1)}, u32[]{:S(2)}, u32[]{:S(2)}) collective-permute-start(bf16[6656,4,128]{2,1,0:T(4,128)(2,1)} %branch_0_fun.30), channel_id=1, source_target_pairs={{0,1},{1,0},{2,3},{3,2},{4,5},{5,4},{6,7},{7,6},{8,9},{9,8},{10,11... | collective-permute-start | bytes 20447240 | tf_op jit(solution)/shard_map/cond/branch_1_fun/cond/branch_0_fun/ppermute | solution.py:754
  205.5 9.2 %branch_0_fun.31 = bf16[6656,4,128]{2,1,0:T(4,128)(2,1)} custom-call(s32[1]{0:T(128)} %get-tuple-element.441.dev_ref, s32[7168]{0:T(1024)S(1)} %copy-done.1, s32[2048]{0:T(1024)S(1)} %get-tuple-element.399.lens_ref, s32[512]{0:T(512)S(1)} %copy-done.26, s32[512]{0:T(512)S(1)} %get-tuple-element.408.src_ref, s32[80]{0:T(128)} %get-tuple-element.412.rest_0_, ...), custom_call_target="tpu_custom_call" | custom-call | tf_op jit(solution)/shard_map/cond/branch_1_fun/cond/branch_0_fun/pallas_call | solution.py:570
  216.3 21.7 %branch_1_fun.27 = (bf16[32,28,128]{2,1,0:T(8,128)(2,1)}, bf16[16384,4,128]{2,1,0:T(4,128)(2,1)}, bf16[16384,4,128]{2,1,0:T(4,128)(2,1)}) custom-call(s32[1]{0:T(128)} %get-tuple-element.781.dev_ref, s32[2048]{0:T(1024)S(1)} %get-tuple-element.782.lens_ref, s32[512]{0:T(512)S(1)} %get-tuple-element.783.src_ref, ...), custom_call_target="tpu_custom_call", output_to_operand_aliasing={{1}: (12, {}), {2}: (13, {})} | custom-call | tf_op jit(solution)/shard_map/cond/branch_1_fun/pallas_call | solution.py:742
  238.4 1.7 copy.31
  (67 shorter events, 24.8 us)
Async XLA Ops:
  10.1 6.6 %copy-start.25 = (s32[512]{0:T(512)S(1)}, s32[512]{0:T(512)}, u32[]{:S(2)}) copy-start(s32[512]{0:T(512)} %dest_ref.1) | copy-start | bytes 6148
  10.1 20.8 %copy-start.63 = (bf16[32,28,128]{2,0,1:T(8,128)(2,1)S(1)}, bf16[32,28,128]{2,0,1:T(8,128)(2,1)}, u32[]{:S(2)}) copy-start(bf16[32,28,128]{2,0,1:T(8,128)(2,1)} %param.26) | copy-start | bytes 688132
  16.6 14.3 %collective-permute-start.172 = (bf16[6912,4,128]{2,1,0:T(4,128)(2,1)}, bf16[6912,4,128]{2,1,0:T(4,128)(2,1)}, u32[]{:S(2)}, u32[]{:S(2)}) collective-permute-start(bf16[6912,4,128]{2,1,0:T(4,128)(2,1)} %get-tuple-element.818), channel_id=1, source_target_pairs={{0,1},{1,0},{2,3},{3,2},{4,5},{5,4},{6,7},{7,6},{8,9},{9,8},{10,11... | collective-permute-start | bytes 21233672 | tf_op jit(solution)/shard_map/ppermute | solution.py:754
  33.3 5.8 %copy-start.26 = (s32[512]{0:T(512)S(1)}, s32[512]{0:T(512)}, u32[]{:S(2)}) copy-start(s32[512]{0:T(512)} %get-tuple-element.400.dest_ref) | copy-start | bytes 6148 | tf_op jit(solution)/shard_map/cond/branch_1_fun/cond
  33.4 5.8 %copy-start.67 = (s32[32]{0:T(128)S(1)}, s32[32]{0:T(128)}, u32[]{:S(2)}) copy-start(s32[32]{0:T(128)} %get-tuple-element.406.lens_ref) | copy-start | bytes 388 | tf_op jit(solution)/shard_map/cond/branch_1_fun/cond
  39.2 15.8 %copy-start.1 = (s32[7168]{0:T(1024)S(1)}, s32[7168]{0:T(1024)}, u32[]{:S(2)}) copy-start(s32[7168]{0:T(1024)} %get-tuple-element.398.meta) | copy-start | bytes 86020 | tf_op jit(solution)/shard_map/cond/branch_1_fun/cond
  44.7 12.0 %collective-permute-start = (bf16[6912,4,128]{2,1,0:T(4,128)(2,1)}, bf16[6912,4,128]{2,1,0:T(4,128)(2,1)}, u32[]{:S(2)}, u32[]{:S(2)}) collective-permute-start(bf16[6912,4,128]{2,1,0:T(4,128)(2,1)} %branch_0_fun.20), channel_id=1, source_target_pairs={{0,1},{1,0},{2,3},{3,2},{4,5},{5,4},{6,7},{7,6},{8,9},{9,8},{10,11... | collective-permute-start | bytes 21233672 | tf_op jit(solution)/shard_map/cond/branch_1_fun/cond/branch_0_fun/ppermute | solution.py:754
  44.8 28.7 %collective-permute-start.1 = (bf16[1112,4,128]{2,1,0:T(4,128)(2,1)}, bf16[1112,4,128]{2,1,0:T(4,128)(2,1)S(1)}, u32[]{:S(2)}, u32[]{:S(2)}) collective-permute-start(bf16[1112,4,128]{2,1,0:T(4,128)(2,1)} %get-tuple-element.404), channel_id=1, source_target_pairs={{0,2},{1,3},{2,0},{3,1},{4,6},{5,7},{6,4},{7,5},{8,10},{9,11},{10,... | collective-permute-start | bytes 3416072 | tf_op jit(solution)/shard_map/cond/branch_1_fun/cond/branch_0_fun/ppermute | solution.py:754
  47.4 28.3 %collective-permute-start.2 = (bf16[1112,4,128]{2,1,0:T(4,128)(2,1)}, bf16[1112,4,128]{2,1,0:T(4,128)(2,1)}, u32[]{:S(2)}, u32[]{:S(2)}) collective-permute-start(bf16[1112,4,128]{2,1,0:T(4,128)(2,1)} %get-tuple-element.416), channel_id=1, source_target_pairs={{0,4},{1,5},{2,6},{3,7},{4,0},{5,1},{6,2},{7,3},{8,12},{9,13},{10,... | collective-permute-start | bytes 3416072 | tf_op jit(solution)/shard_map/cond/branch_1_fun/cond/branch_0_fun/ppermute | solution.py:754
  47.4 28.3 %collective-permute-start.3 = (bf16[1112,4,128]{2,1,0:T(4,128)(2,1)}, bf16[1112,4,128]{2,1,0:T(4,128)(2,1)}, u32[]{:S(2)}, u32[]{:S(2)}) collective-permute-start(bf16[1112,4,128]{2,1,0:T(4,128)(2,1)} %get-tuple-element.417), channel_id=1, source_target_pairs={{0,8},{1,9},{2,10},{3,11},{4,12},{5,13},{6,14},{7,15},{8,0},{9,1},... | collective-permute-start | bytes 3416072 | tf_op jit(solution)/shard_map/cond/branch_1_fun/cond/branch_0_fun/ppermute | solution.py:754
  62.4 35.5 %collective-permute-start.4 = (bf16[1112,4,128]{2,1,0:T(4,128)(2,1)}, bf16[1112,4,128]{2,1,0:T(4,128)(2,1)S(1)}, u32[]{:S(2)}, u32[]{:S(2)}) collective-permute-start(bf16[1112,4,128]{2,1,0:T(4,128)(2,1)} %get-tuple-element.414), channel_id=1, source_target_pairs={{0,2},{1,3},{2,0},{3,1},{4,6},{5,7},{6,4},{7,5},{8,10},{9,11},{10,... | collective-permute-start | bytes 3416072 | tf_op jit(solution)/shard_map/cond/branch_1_fun/cond/branch_0_fun/ppermute | solution.py:754
  66.3 33.7 %collective-permute-start.5 = (bf16[1112,4,128]{2,1,0:T(4,128)(2,1)}, bf16[1112,4,128]{2,1,0:T(4,128)(2,1)S(1)}, u32[]{:S(2)}, u32[]{:S(2)}) collective-permute-start(bf16[1112,4,128]{2,1,0:T(4,128)(2,1)} %get-tuple-element.420), channel_id=1, source_target_pairs={{0,4},{1,5},{2,6},{3,7},{4,0},{5,1},{6,2},{7,3},{8,12},{9,13},{10,... | collective-permute-start | bytes 3416072 | tf_op jit(solution)/shard_map/cond/branch_1_fun/cond/branch_0_fun/ppermute | solution.py:754
  73.5 2.1 copy-start.23
  73.5 26.5 %collective-permute-start.6 = (bf16[1112,4,128]{2,1,0:T(4,128)(2,1)}, bf16[1112,4,128]{2,1,0:T(4,128)(2,1)}, u32[]{:S(2)}, u32[]{:S(2)}) collective-permute-start(bf16[1112,4,128]{2,1,0:T(4,128)(2,1)} %get-tuple-element.421), channel_id=1, source_target_pairs={{0,8},{1,9},{2,10},{3,11},{4,12},{5,13},{6,14},{7,15},{8,0},{9,1},... | collective-permute-start | bytes 3416072 | tf_op jit(solution)/shard_map/cond/branch_1_fun/cond/branch_0_fun/ppermute | solution.py:754
  81.6 40.7 %collective-permute-start.7 = (bf16[1112,4,128]{2,1,0:T(4,128)(2,1)}, bf16[1112,4,128]{2,1,0:T(4,128)(2,1)S(1)}, u32[]{:S(2)}, u32[]{:S(2)}) collective-permute-start(bf16[1112,4,128]{2,1,0:T(4,128)(2,1)} %get-tuple-element.418), channel_id=1, source_target_pairs={{0,2},{1,3},{2,0},{3,1},{4,6},{5,7},{6,4},{7,5},{8,10},{9,11},{10,... | collective-permute-start | bytes 3416072 | tf_op jit(solution)/shard_map/cond/branch_1_fun/cond/branch_0_fun/ppermute | solution.py:754
  83.2 41.2 %collective-permute-start.8 = (bf16[1112,4,128]{2,1,0:T(4,128)(2,1)}, bf16[1112,4,128]{2,1,0:T(4,128)(2,1)}, u32[]{:S(2)}, u32[]{:S(2)}) collective-permute-start(bf16[1112,4,128]{2,1,0:T(4,128)(2,1)} %get-tuple-element.424), channel_id=1, source_target_pairs={{0,4},{1,5},{2,6},{3,7},{4,0},{5,1},{6,2},{7,3},{8,12},{9,13},{10,... | collective-permute-start | bytes 3416072 | tf_op jit(solution)/shard_map/cond/branch_1_fun/cond/branch_0_fun/ppermute | solution.py:754
  97.9 26.5 %collective-permute-start.9 = (bf16[1112,4,128]{2,1,0:T(4,128)(2,1)}, bf16[1112,4,128]{2,1,0:T(4,128)(2,1)}, u32[]{:S(2)}, u32[]{:S(2)}) collective-permute-start(bf16[1112,4,128]{2,1,0:T(4,128)(2,1)} %get-tuple-element.425), channel_id=1, source_target_pairs={{0,8},{1,9},{2,10},{3,11},{4,12},{5,13},{6,14},{7,15},{8,0},{9,1},... | collective-permute-start | bytes 3416072 | tf_op jit(solution)/shard_map/cond/branch_1_fun/cond/branch_0_fun/ppermute | solution.py:754
  107.0 39.7 %collective-permute-start.10 = (bf16[1112,4,128]{2,1,0:T(4,128)(2,1)}, bf16[1112,4,128]{2,1,0:T(4,128)(2,1)S(1)}, u32[]{:S(2)}, u32[]{:S(2)}) collective-permute-start(bf16[1112,4,128]{2,1,0:T(4,128)(2,1)} %get-tuple-element.422), channel_id=1, source_target_pairs={{0,2},{1,3},{2,0},{3,1},{4,6},{5,7},{6,4},{7,5},{8,10},{9,11},{10,... | collective-permute-start | bytes 3416072 | tf_op jit(solution)/shard_map/cond/branch_1_fun/cond/branch_0_fun/ppermute | solution.py:754
  108.6 40.1 %collective-permute-start.11 = (bf16[1112,4,128]{2,1,0:T(4,128)(2,1)}, bf16[1112,4,128]{2,1,0:T(4,128)(2,1)S(1)}, u32[]{:S(2)}, u32[]{:S(2)}) collective-permute-start(bf16[1112,4,128]{2,1,0:T(4,128)(2,1)} %get-tuple-element.428), channel_id=1, source_target_pairs={{0,4},{1,5},{2,6},{3,7},{4,0},{5,1},{6,2},{7,3},{8,12},{9,13},{10,... | collective-permute-start | bytes 3416072 | tf_op jit(solution)/shard_map/cond/branch_1_fun/cond/branch_0_fun/ppermute | solution.py:754
  122.3 2.1 copy-start.46
  122.3 26.5 %collective-permute-start.12 = (bf16[1112,4,128]{2,1,0:T(4,128)(2,1)}, bf16[1112,4,128]{2,1,0:T(4,128)(2,1)}, u32[]{:S(2)}, u32[]{:S(2)}) collective-permute-start(bf16[1112,4,128]{2,1,0:T(4,128)(2,1)} %get-tuple-element.429), channel_id=1, source_target_pairs={{0,8},{1,9},{2,10},{3,11},{4,12},{5,13},{6,14},{7,15},{8,0},{9,1},... | collective-permute-start | bytes 3416072 | tf_op jit(solution)/shard_map/cond/branch_1_fun/cond/branch_0_fun/ppermute | solution.py:754
  130.8 40.3 %collective-permute-start.13 = (bf16[1112,4,128]{2,1,0:T(4,128)(2,1)}, bf16[1112,4,128]{2,1,0:T(4,128)(2,1)S(1)}, u32[]{:S(2)}, u32[]{:S(2)}) collective-permute-start(bf16[1112,4,128]{2,1,0:T(4,128)(2,1)} %get-tuple-element.426), channel_id=1, source_target_pairs={{0,2},{1,3},{2,0},{3,1},{4,6},{5,7},{6,4},{7,5},{8,10},{9,11},{10,... | collective-permute-start | bytes 3416072 | tf_op jit(solution)/shard_map/cond/branch_1_fun/cond/branch_0_fun/ppermute | solution.py:754
  132.6 40.6 %collective-permute-start.14 = (bf16[1112,4,128]{2,1,0:T(4,128)(2,1)}, bf16[1112,4,128]{2,1,0:T(4,128)(2,1)}, u32[]{:S(2)}, u32[]{:S(2)}) collective-permute-start(bf16[1112,4,128]{2,1,0:T(4,128)(2,1)} %get-tuple-element.435), channel_id=1, source_target_pairs={{0,4},{1,5},{2,6},{3,7},{4,0},{5,1},{6,2},{7,3},{8,12},{9,13},{10,... | collective-permute-start | bytes 3416072 | tf_op jit(solution)/shard_map/cond/branch_1_fun/cond/branch_0_fun/ppermute | solution.py:754
  146.7 2.1 copy-start.45
  146.7 26.5 %collective-permute-start.15 = (bf16[1112,4,128]{2,1,0:T(4,128)(2,1)}, bf16[1112,4,128]{2,1,0:T(4,128)(2,1)}, u32[]{:S(2)}, u32[]{:S(2)}) collective-permute-start(bf16[1112,4,128]{2,1,0:T(4,128)(2,1)} %get-tuple-element.436), channel_id=1, source_target_pairs={{0,8},{1,9},{2,10},{3,11},{4,12},{5,13},{6,14},{7,15},{8,0},{9,1},... | collective-permute-start | bytes 3416072 | tf_op jit(solution)/shard_map/cond/branch_1_fun/cond/branch_0_fun/ppermute | solution.py:754
  156.1 38.8 %collective-permute-start.16 = (bf16[1112,4,128]{2,1,0:T(4,128)(2,1)}, bf16[1112,4,128]{2,1,0:T(4,128)(2,1)S(1)}, u32[]{:S(2)}, u32[]{:S(2)}) collective-permute-start(bf16[1112,4,128]{2,1,0:T(4,128)(2,1)} %get-tuple-element.430), channel_id=1, source_target_pairs={{0,2},{1,3},{2,0},{3,1},{4,6},{5,7},{6,4},{7,5},{8,10},{9,11},{10,... | collective-permute-start | bytes 3416072 | tf_op jit(solution)/shard_map/cond/branch_1_fun/cond/branch_0_fun/ppermute | solution.py:754
  157.7 38.7 %collective-permute-start.17 = (bf16[1112,4,128]{2,1,0:T(4,128)(2,1)}, bf16[1112,4,128]{2,1,0:T(4,128)(2,1)S(1)}, u32[]{:S(2)}, u32[]{:S(2)}) collective-permute-start(bf16[1112,4,128]{2,1,0:T(4,128)(2,1)} %get-tuple-element.439), channel_id=1, source_target_pairs={{0,4},{1,5},{2,6},{3,7},{4,0},{5,1},{6,2},{7,3},{8,12},{9,13},{10,... | collective-permute-start | bytes 3416072 | tf_op jit(solution)/shard_map/cond/branch_1_fun/cond/branch_0_fun/ppermute | solution.py:754
  171.1 2.1 copy-start.61
  171.1 26.5 %collective-permute-start.18 = (bf16[1112,4,128]{2,1,0:T(4,128)(2,1)}, bf16[1112,4,128]{2,1,0:T(4,128)(2,1)}, u32[]{:S(2)}, u32[]{:S(2)}) collective-permute-start(bf16[1112,4,128]{2,1,0:T(4,128)(2,1)} %get-tuple-element.440), channel_id=1, source_target_pairs={{0,8},{1,9},{2,10},{3,11},{4,12},{5,13},{6,14},{7,15},{8,0},{9,1},... | collective-permute-start | bytes 3416072 | tf_op jit(solution)/shard_map/cond/branch_1_fun/cond/branch_0_fun/ppermute | solution.py:754
  178.3 36.4 %collective-permute-start.19 = (bf16[6656,4,128]{2,1,0:T(4,128)(2,1)}, bf16[6656,4,128]{2,1,0:T(4,128)(2,1)}, u32[]{:S(2)}, u32[]{:S(2)}) collective-permute-start(bf16[6656,4,128]{2,1,0:T(4,128)(2,1)} %branch_0_fun.28), channel_id=1, source_target_pairs={{0,1},{1,0},{2,3},{3,2},{4,5},{5,4},{6,7},{7,6},{8,9},{9,8},{10,11... | collective-permute-start | bytes 20447240 | tf_op jit(solution)/shard_map/cond/branch_1_fun/cond/branch_0_fun/ppermute | solution.py:754
  194.9 2.7 %copy-start.60 = (bf16[1112,4,128]{2,1,0:T(4,128)(2,1)}, bf16[1112,4,128]{2,1,0:T(4,128)(2,1)S(1)}, u32[]{:S(2)}) copy-start(bf16[1112,4,128]{2,1,0:T(4,128)(2,1)S(1)} %collective-permute-done.16.rest_13_) | copy-start | bytes 3416068 | tf_op jit(solution)/shard_map/cond/branch_1_fun/cond
  202.8 13.6 %collective-permute-start.20 = (bf16[6656,4,128]{2,1,0:T(4,128)(2,1)}, bf16[6656,4,128]{2,1,0:T(4,128)(2,1)}, u32[]{:S(2)}, u32[]{:S(2)}) collective-permute-start(bf16[6656,4,128]{2,1,0:T(4,128)(2,1)} %branch_0_fun.30), channel_id=1, source_target_pairs={{0,1},{1,0},{2,3},{3,2},{4,5},{5,4},{6,7},{7,6},{8,9},{9,8},{10,11... | collective-permute-start | bytes 20447240 | tf_op jit(solution)/shard_map/cond/branch_1_fun/cond/branch_0_fun/ppermute | solution.py:754
  (6 other events, 7.3 us)
where the time goes:
time: 242 us; the launch traced here: 240 us
  Pallas kernels  128 us (53%)
  waiting for transfers between devices  76.3 us (32%)
  starting transfers between devices  26.3 us (11%)
  local copies, waits for them, and re-layouts  7.11 us (3%)
    ppermute x22, waiting for transfers between devices, swap(): return lax.ppermute(x, 'dp', [(i, i ^ mask) for i in range(DEVS)])  76.3 us
    pallas_call x6, Pallas kernels, pack(): local_call(functools.partial(pack_kernel, beta, step, cap), out_shape=[ro...  36.1 us
    pallas_call x4, Pallas kernels, post_pack(): local_call(functools.partial(post_kernel, beta, other), out_shape=rows_of...  28.5 us
    ppermute x22, starting transfers between devices, swap(): return lax.ppermute(x, 'dp', [(i, i ^ mask) for i in range(DEVS)])  26.3 us
    pallas_call x1, Pallas kernels, finish(): local_call(finish_kernel, out_shape=[jax.ShapeDtypeStruct((SLOTS, HEADS,...  21.7 us
    pallas_call x1, Pallas kernels, make_plan(): pl.pallas_call(plan_kernel, out_shape=jax.ShapeDtypeStruct((META_ROWS, LA...  12.9 us
    pallas_call x2, Pallas kernels, pre_pack(): local_call(functools.partial(pre_kernel, beta, with_src), out_shape=out,...  12 us
    pallas_call x1, Pallas kernels, gather_lens(): pl.pallas_call(gather_kernel, out_shape=jax.ShapeDtypeStruct((DEVS, 1, LA...  8.26 us
  transfers between devices with their start and end apart: 22, of which 16 were waited for; matrix products, arithmetic and copies ran while one was open for 0% of the time, Pallas kernels for 33%

commit v1 on v0

--- a/solution.py
+++ b/solution.py
@@ -14,25 +14,26 @@
 DEVS, SLOTS, TOTAL = 16, 32, 512
 CHIPS, CHIP_SLOTS = 8, 64
 DESTS = range(1, CHIPS)
-ROWS = 512
-HEADS, KV, DIM, GROUP = 28, 4, 128, 7
+ROWS = 256
+HEADS, KV, TILE, DIM, GROUP = 28, 4, 8, 128, 7
+PADDED = 32
 LANES = 128
 BATCHES = (0, 1)
-PRE = 6912
-POST = 6656
+PRE = 3456
+POST = 3328
 HALF = ROWS // 2
-CLASSES = (2224, 2552, 2752, 2984, 3176, 3400, 3592, 4600)
-ITERS = 12
-FIRST_STEP, SHRINK = 1.5, 15 ** (-1 / 11)
+CLASSES = (1088, 1208, 1312, 1424, 1552, 1648, 1816, 2304)
+ITERS, FIRST_STEP, SHRINK, MOMENTUM = 10, 0.675, 0.838, 0.9
 LAST = jnp.iinfo(jnp.int32).max
 VMEM_LIMIT = 62914560
 TABLES = 40
+LINKS = 3
 
 
 def make_options():
     found = []
     for b in DESTS:
-        dims = [k for k in range(3) if (b >> k) & 1]
+        dims = [k for k in range(LINKS) if (b >> k) & 1]
         mine = []
         for steps in itertools.combinations(range(3), len(dims)):
             for order in itertools.permutations(dims):
@@ -54,8 +55,8 @@
 
 def make_flows():
     flows = {}
-    for step in range(3):
-        for k in range(3):
+    for step in range(LINKS):
+        for k in range(LINKS):
             runs = []
             for o, (_, hops) in enumerate(OPTIONS):
                 for h, (st, place, kk) in enumerate(hops):
@@ -107,7 +108,7 @@
 
     lens = lens_ref[...].reshape(CHIPS, 2 * LANES)
     lens = jnp.where(lane < SLOTS, lens[:, :LANES], pltpu.roll(lens[:, LANES:], SLOTS, 1))
-    lens = jnp.where(lane < CHIP_SLOTS, lens, 0)
+    lens = jnp.where(lane < CHIP_SLOTS, (lens + 1) >> 1, 0)
     flat = dest_ref[...]
     turned = pltpu.roll(flat, CHIP_SLOTS, 1)
     to = jnp.concatenate([(turned if c & 1 else flat)[c >> 1:(c >> 1) + 1] for c in range(CHIPS)], axis=0)
@@ -159,18 +160,21 @@
     weight = norm(jnp.ones(shape, F32))
 
     def improve(_, carry):
-        weight, best, best_top, size = carry
+        weight, best, best_top, drift, size = carry
         loads = link_loads(weight * both, plain)
         top = top_of(loads)
         better = top < best_top
         best = jnp.where(better, weight, best)
         best_top = jnp.where(better, top, best_top)
         price = loads / jnp.maximum(top, 1.0)
-        for _ in BITS:
-            price = price * price
-        return norm(weight * jnp.exp(-size * path_cost(price))), best, best_top, size * SHRINK
-
-    start = (weight, weight, jnp.full((1, 1), 3e38, F32), jnp.full((1, 1), FIRST_STEP, F32))
+        price = price * price
+        cost = path_cost(price * price * price)
+        drift = MOMENTUM * drift + cost
+        weight = norm(weight * jnp.exp(-size * (MOMENTUM * drift + cost)))
+        return weight, best, best_top, drift, size * SHRINK
+
+    one = jnp.ones((1, 1), F32)
+    start = (weight, weight, 3e38 * one, jnp.zeros(shape, F32), FIRST_STEP * one)
     best = lax.fori_loop(0, ITERS, improve, start)[1]
 
     pick = jnp.zeros((1, 1), I32)
@@ -243,9 +247,13 @@
     return lens_ref[(slot >> 5) * LANES + (slot & 31)]
 
 
+def pairs_of(m):
+    return (m + 1) >> 1
+
+
 def part_of(m, beta):
-    early = (m + 1) >> 1
-    return (0, early)[beta], (early, m - early)[beta]
+    early = (m + 3) >> 2
+    return (0, early)[beta], (early, pairs_of(m) - early)[beta]
 
 
 def row_copy(src, s0, dst, d0, n, sem):
@@ -279,7 +287,7 @@
 
 
 def rows_of(n, dtype=BF):
-    return jax.ShapeDtypeStruct((n, KV, DIM), dtype)
+    return jax.ShapeDtypeStruct((n, TILE, DIM), dtype)
 
 
 def local_call(kernel, **kwargs):
@@ -327,7 +335,7 @@
     got = local_call(
         functools.partial(pre_kernel, beta, with_src),
         out_shape=out, out_specs=specs, in_specs=[SMEM] * 3 + [ANY] * 2,
-        scratch_shapes=[pltpu.VMEM((SLOTS * HALF, KV, DIM), BF), pltpu.SemaphoreType.DMA],
+        scratch_shapes=[pltpu.VMEM((SLOTS * HALF, TILE, DIM), BF), pltpu.SemaphoreType.DMA],
     )(dev, lens, dest, k, v)
     return got if with_src else got[0]
 
@@ -359,7 +367,7 @@
     plan = Table(meta, chip, beta)
     used = []
     count = I32(0)
-    for k in range(3):
+    for k in range(LINKS):
         where = I32(0)
         spans = {}
         for place, o, _ in FLOWS[step, k]:
@@ -395,7 +403,7 @@
                     if h + 1 < len(hops) and hops[h + 1][0] == step:
                         came[v, o] = (st, kk, at, n)
                     at = at + n
-        for k in range(3):
+        for k in range(LINKS):
             for place, o, h in FLOWS[step, k]:
                 if place == 0:
                     continue
@@ -418,7 +426,7 @@
         @pl.when(b > 0)
         def _():
             begin = plan.start(slot)
-            for k in range(3):
+            for k in range(LINKS):
                 lo = jnp.maximum(begin, table_lo[b * 3 + k])
                 hi = jnp.minimum(begin + n, table_hi[b * 3 + k])
                 size = hi - lo
@@ -442,11 +450,11 @@
 
     lax.fori_loop(0, 64, one, I32(0))
     drain(stage, count, sem)
-    for k in range(3):
+    for k in range(LINKS):
         @pl.when(used[k] > 0)
         def _(k=k):
             row_copy(stage, k * cap, outs[k], 0, used[k], sem_out.at[k]).start()
-    for k in range(3):
+    for k in range(LINKS):
         @pl.when(used[k] > 0)
         def _(k=k):
             row_copy(stage, k * cap, outs[k], 0, used[k], sem_out.at[k]).wait()
@@ -459,7 +467,7 @@
         functools.partial(pack_kernel, beta, step, cap),
         out_shape=[rows_of(cap)] * 3, out_specs=[ANY] * 3,
         in_specs=[SMEM] * 4 + [ANY] * (3 + len(recv)),
-        scratch_shapes=[pltpu.VMEM((3 * cap, KV, DIM), BF)] + [pltpu.SMEM((TABLES,), I32)] * 3
+        scratch_shapes=[pltpu.VMEM((3 * cap, TILE, DIM), BF)] + [pltpu.SMEM((TABLES,), I32)] * 3
         + [pltpu.SemaphoreType.DMA, pltpu.SemaphoreType.DMA((3,))],
     )(dev, meta, lens, dest, k, v, pre, *recv)
 
@@ -524,7 +532,11 @@
 
 
 def post_kernel(beta, other, dev_ref, meta, lens_ref, dest_ref, src_ref, *rest):
-    tables, (k_ref, v_ref, pre_ref, *recv), (out_ref, stage, pre_at, sem) = rest[:4], rest[4:16], rest[16:]
+    tables, (k_ref, v_ref, pre_ref, *recv), rest = rest[:4], rest[4:16], rest[16:]
+    if other:
+        out_ref, stage, sem = rest
+    else:
+        ko_ref, vo_ref, stage, pre_at, sem, sem_out = rest[2:]
     dev = dev_ref[0]
     chip, core = dev >> 1, dev & 1
     plan = Table(meta, chip, beta)
@@ -562,47 +574,77 @@
 
     total = lax.fori_loop(0, SLOTS, one, I32(0))
     drain(stage, total, sem)
-    flush(stage, 0, out_ref, total, sem)
-
-
-def post_pack(beta, other, scalars, tables, k, v, pre, recv):
-    recv = [recv[q // 3, q % 3] for q in range(9)]
+    if other:
+        flush(stage, 0, out_ref, total, sem)
+        return
+
+    def put(j, q):
+        slot = src_ref[target * SLOTS + j]
+        start, n = part_of(length(lens_ref, slot), beta)
+        n = jnp.where((slot >> 5) == target, 0, n)
+
+        @pl.when(n > 0)
+        def _():
+            for c, out in enumerate((ko_ref, vo_ref)):
+                @pl.when(core == c)
+                def _(out=out):
+                    row_copy(stage, q, out, j * ROWS + start, n, sem_out).start()
+
+        return q + n
+
+    lax.fori_loop(0, SLOTS, put, I32(0))
+    drain(stage, total, sem_out)
+
+
+def post_pack(beta, scalars, tables, k, v, pre, recv):
     return local_call(
-        functools.partial(post_kernel, beta, other),
+        functools.partial(post_kernel, beta, True),
         out_shape=rows_of(POST), out_specs=ANY,
         in_specs=[SMEM] * 9 + [ANY] * 12,
-        scratch_shapes=[pltpu.VMEM((POST, KV, DIM), BF), pltpu.SMEM((SLOTS,), I32), pltpu.SemaphoreType.DMA],
-    )(*scalars, *tables, k, v, pre, *recv)
-
-
-ZEROS = 480
+        scratch_shapes=[pltpu.VMEM((POST, TILE, DIM), BF), pltpu.SemaphoreType.DMA],
+    )(*scalars, *tables, k, v, pre, *[recv[q // LINKS, q % LINKS] for q in range(LINKS * LINKS)])
+
+
+def land(beta, scalars, tables, k, v, pre, recv, outs):
+    in_specs = [SMEM] * 9 + [ANY] * 12
+    return local_call(
+        functools.partial(post_kernel, beta, False),
+        out_shape=[rows_of(SLOTS * ROWS)] * 2, out_specs=[ANY] * 2, in_specs=in_specs + [ANY] * 2,
+        input_output_aliases={len(in_specs): 0, len(in_specs) + 1: 1},
+        scratch_shapes=[pltpu.VMEM((POST, TILE, DIM), BF), pltpu.SMEM((SLOTS,), I32)] + [pltpu.SemaphoreType.DMA] * 2,
+    )(*scalars, *tables, k, v, pre, *[recv[q // LINKS, q % LINKS] for q in range(LINKS * LINKS)], *outs)
+
+
+ZEROS = 256
 
 
 def zeros_kernel(dev_ref, lens_ref, src_ref, q_ref, ko_ref, vo_ref, lens_out, q_out, zeros, sem):
     dev = dev_ref[0]
 
     def clear(t, _):
-        zeros[pl.ds(t * SLOTS, SLOTS)] = jnp.zeros((SLOTS, KV, DIM), BF)
+        zeros[pl.ds(t * SLOTS, SLOTS)] = jnp.zeros((SLOTS, TILE, DIM), BF)
         return 0
 
     lax.fori_loop(0, ZEROS // SLOTS, clear, 0)
 
     def each(wait, j, _):
         m = length(lens_ref, src_ref[dev * SLOTS + j])
-        n = ROWS - 1 - m
+        behind = (m >> 1) + 1
+        n = ROWS - behind
         if not wait:
             lens_out[j] = m + 1
 
         @pl.when(n > 0)
         def _():
             for q, out in enumerate((ko_ref, vo_ref)):
-                copy = row_copy(zeros, 0, out, j * ROWS + m + 1, n, sem.at[q, j])
+                copy = row_copy(zeros, 0, out, j * ROWS + behind, n, sem.at[q, j])
                 copy.wait() if wait else copy.start()
 
         return 0
 
     lax.fori_loop(0, SLOTS, functools.partial(each, False), 0)
-    q_out[...] = q_ref[...]
+    q_out[...] = jnp.zeros_like(q_out)
+    q_out[:, :HEADS] = q_ref[...]
     lax.fori_loop(0, SLOTS, functools.partial(each, True), 0)
 
 
@@ -610,18 +652,18 @@
     return local_call(
         zeros_kernel,
         out_shape=[rows_of(SLOTS * ROWS)] * 2 + [jax.ShapeDtypeStruct((SLOTS,), I32),
-                                               jax.ShapeDtypeStruct(query.shape, BF)],
+                                               jax.ShapeDtypeStruct((SLOTS, PADDED, DIM), BF)],
         out_specs=[ANY, ANY, SMEM, VMEM], in_specs=[SMEM] * 3 + [VMEM],
-        scratch_shapes=[pltpu.VMEM((ZEROS, KV, DIM), BF), pltpu.SemaphoreType.DMA((2, SLOTS))],
+        scratch_shapes=[pltpu.VMEM((ZEROS, TILE, DIM), BF), pltpu.SemaphoreType.DMA((2, SLOTS))],
     )(dev, lens, src, query)
 
 
-N_BUF, AHEAD, UNROLL = 12, 8, 2
+N_BUF, AHEAD, UNROLL = 12, 8, 4
 
 
 def finish_kernel(dev_ref, lens_ref, src_ref, k_ref, v_ref, *rest):
-    land, post = rest[0:2], rest[2:4]
-    q_ref, kn_ref, vn_ref, _, _, attn_ref, ko_ref, vo_ref, bufs, cols, moved_at, sem_in, sem_out = rest[4:]
+    post = rest[0:2]
+    q_ref, kn_ref, vn_ref, _, _, attn_ref, ko_ref, vo_ref, bufs, cols, moved_at, sem_in, sem_out = rest[2:]
     dev = dev_ref[0]
     core = dev & 1
 
@@ -646,44 +688,48 @@
         @pl.when((slot >> 5) == dev)
         def _():
             home = (slot & 31) * ROWS
-            row_copy(k_ref, home, bufs.at[0, buf], 0, m, sem_in.at[0, buf]).start()
-            row_copy(v_ref, home, bufs.at[1, buf], 0, m, sem_in.at[1, buf]).start()
+            row_copy(k_ref, home, bufs.at[0, buf], 0, pairs_of(m), sem_in.at[0, buf]).start()
+            row_copy(v_ref, home, bufs.at[1, buf], 0, pairs_of(m), sem_in.at[1, buf]).start()
 
         @pl.when((slot >> 5) != dev)
         def _():
+            start_copy(core, False, ko_ref, vo_ref, j * ROWS, bufs.at[core, buf], 0, pairs_of(m), sem_in.at[core, buf])
             for beta in BATCHES:
                 start, n = part_of(m, beta)
-                at = moved_at[SLOTS * beta + j]
-                for ref, q in ((land[beta], core), (post[beta], 1 - core)):
-                    row_copy(ref, at, bufs.at[q, buf], start, n, sem_in.at[q, buf]).start()
+                row_copy(post[beta], moved_at[SLOTS * beta + j], bufs.at[1 - core, buf], start, n,
+                         sem_in.at[1 - core, buf]).start()
 
     def emit(j, wait):
-        _, m = source(j)
+        slot, m = source(j)
         buf = lax.rem(j, N_BUF)
         for q, out in enumerate((ko_ref, vo_ref)):
-            copy = row_copy(bufs.at[q, buf], 0, out, j * ROWS, m + 1, sem_out.at[q, buf])
+            here = ((slot >> 5) != dev) & (core == q)
+            end = m >> 1
+            first = jnp.where(here, end, 0)
+            copy = row_copy(bufs.at[q, buf], first, out, j * ROWS + first, end + 1 - first, sem_out.at[q, buf])
             copy.wait() if wait else copy.start()
 
     def clear(t, _):
-        bufs[1, t // KV, pl.ds((t % KV) * DIM, DIM)] = jnp.zeros((DIM, KV, DIM), BF)
+        bufs[1, t // 2, pl.ds((t % 2) * DIM, DIM)] = jnp.zeros((DIM, TILE, DIM), BF)
         return 0
 
-    lax.fori_loop(0, KV * N_BUF, clear, 0)
+    lax.fori_loop(0, 2 * N_BUF, clear, 0)
 
     def begin(j, _):
         fetch(j)
         return 0
 
     lax.fori_loop(0, AHEAD, begin, 0)
-    head = lax.broadcasted_iota(I32, (HEADS, LANES), 0) // GROUP
-    col = lax.broadcasted_iota(I32, (HEADS, LANES), 1)
+    half = lax.broadcasted_iota(I32, (TILE, DIM), 0) // KV
+    head = lax.broadcasted_iota(I32, (PADDED, LANES), 0) // GROUP
+    col = lax.broadcasted_iota(I32, (PADDED, LANES), 1)
     mine = jnp.where(head == (col & (KV - 1)), col, LAST // 2)
 
     def number(t, _):
         cols[:, pl.ds(pl.multiple_of(t * LANES, LANES), LANES)] = mine + t * LANES
         return 0
 
-    lax.fori_loop(0, KV * ROWS // LANES, number, 0)
+    lax.fori_loop(0, TILE * ROWS // LANES, number, 0)
 
     def some(jj, _):
         def prefetch(u, _):
@@ -706,8 +752,10 @@
             _, m = source(j)
             buf = lax.rem(j, N_BUF)
             for q, new in enumerate((kn_ref, vn_ref)):
-                row_copy(k_ref, 0, bufs.at[q, buf], 0, m, sem_in.at[q, buf]).wait()
-                bufs[q, buf, m] = new[j]
+                row_copy(k_ref, 0, bufs.at[q, buf], 0, pairs_of(m), sem_in.at[q, buf]).wait()
+                both = jnp.concatenate([new[j], new[j]], axis=0)
+                kept = jnp.where(half < (m & 1), bufs[q, buf, m >> 1], jnp.zeros_like(both))
+                bufs[q, buf, m >> 1] = jnp.where(half == (m & 1), both, kept)
             emit(j, False)
             return 0
 
@@ -715,16 +763,16 @@
         scores = []
         for u in range(UNROLL):
             j = UNROLL * jj + u
-            kk = bufs[0, lax.rem(j, N_BUF)].reshape(KV * ROWS, DIM)
+            kk = bufs[0, lax.rem(j, N_BUF)].reshape(TILE * ROWS, DIM)
             s = lax.dot_general(q_ref[j], kk, (((1,), (1,)), ((), ())), preferred_element_type=F32)
             scores.append(jnp.where(cols[...] < KV * (source(j)[1] + 1), s * (DIM ** -0.5), -1e30))
         for u, s in enumerate(scores):
             j = UNROLL * jj + u
             p = jnp.exp(s - jnp.max(s, axis=1, keepdims=True))
             total = jnp.sum(p, axis=1, keepdims=True)
-            vv = bufs[1, lax.rem(j, N_BUF)].reshape(KV * ROWS, DIM)
+            vv = bufs[1, lax.rem(j, N_BUF)].reshape(TILE * ROWS, DIM)
             acc = jnp.dot(p.astype(BF), vv, preferred_element_type=F32)
-            attn_ref[j] = (acc / total).astype(BF)
+            attn_ref[j] = (acc / total)[:HEADS].astype(BF)
         return 0
 
     lax.fori_loop(0, SLOTS // UNROLL, some, 0)
@@ -736,17 +784,17 @@
     lax.fori_loop(SLOTS - N_BUF, SLOTS, wait_out, 0)
 
 
-def finish(scalars, k, v, land, post, query, k_new, v_new, outs):
-    in_specs = [SMEM] * 3 + [ANY] * 6 + [VMEM] * 3
+def finish(scalars, k, v, post, query, k_new, v_new, outs):
+    in_specs = [SMEM] * 3 + [ANY] * 4 + [VMEM] * 3
     dev, _, lens, _, src = scalars
     attn, ko, vo = local_call(
         finish_kernel,
         out_shape=[jax.ShapeDtypeStruct((SLOTS, HEADS, DIM), BF)] + [rows_of(SLOTS * ROWS)] * 2,
         out_specs=[VMEM, ANY, ANY], in_specs=in_specs + [ANY] * 2,
         input_output_aliases={len(in_specs): 1, len(in_specs) + 1: 2},
-        scratch_shapes=[pltpu.VMEM((2, N_BUF, ROWS, KV, DIM), BF), pltpu.VMEM((HEADS, KV * ROWS), I32),
+        scratch_shapes=[pltpu.VMEM((2, N_BUF, ROWS, TILE, DIM), BF), pltpu.VMEM((PADDED, TILE * ROWS), I32),
                         pltpu.SMEM((2 * SLOTS,), I32)] + [pltpu.SemaphoreType.DMA((2, N_BUF))] * 2,
-    )(dev, lens, src, k, v, *land, *post, query, k_new, v_new, *outs)
+    )(dev, lens, src, k, v, *post, query, k_new, v_new, *outs)
     return attn, ko, vo
 
 
@@ -763,7 +811,7 @@
     cap = caps_of(rows)
     recv, pre = [{}, {}], [pre0, None]
     turn = dev
-    for step in range(3):
+    for step in range(LINKS):
         for beta in BATCHES:
             if step == 0 and beta == 1:
                 pre_send = pre_pack(1, False, turn, my_lens, dest, k, v)
@@ -773,16 +821,16 @@
                 turn = after(dev, tables[0])
             sends = pack(beta, step, cap, (turn, *scalars[1:]), k, v, pre[beta], recv[beta])
             turn = after(dev, sends[0])
-            for dim in range(3):
+            for dim in range(LINKS):
                 recv[beta][step, dim] = swap(sends[dim], 2 << dim)
-    land, post = [], []
+    post, outs = [], (ko, vo)
     for beta in BATCHES:
-        packed = post_pack(beta, True, (turn, *scalars[1:]), tables, k, v, pre[beta], recv[beta])
+        packed = post_pack(beta, (turn, *scalars[1:]), tables, k, v, pre[beta], recv[beta])
         turn = after(dev, packed)
         post.append(swap(packed, 1))
-        land.append(post_pack(beta, False, (turn, *scalars[1:]), tables, k, v, pre[beta], recv[beta]))
-        turn = after(dev, land[-1])
-    return *land, *post, ko, vo, query, lens_out
+        outs = land(beta, (turn, *scalars[1:]), tables, k, v, pre[beta], recv[beta], outs)
+        turn = after(dev, outs[0])
+    return *post, *outs, query, lens_out
 
 
 def take_kernel(owner_ref, dev_ref, src_ref, kh, vh, _, __, ka, va, stage, sem):
@@ -810,7 +858,7 @@
         ka, va = local_call(
             take_kernel, out_shape=[rows_of(SLOTS * ROWS)] * 2, out_specs=[ANY] * 2,
             in_specs=[SMEM] * 3 + [ANY] * 4, input_output_aliases={5: 0, 6: 1},
-            scratch_shapes=[pltpu.VMEM((ROWS, KV, DIM), BF), pltpu.SemaphoreType.DMA],
+            scratch_shapes=[pltpu.VMEM((ROWS, TILE, DIM), BF), pltpu.SemaphoreType.DMA],
         )(owner, dev, src, *carry)
         return *[lax.ppermute(x, 'dp', shift) for x in carry[:2]], ka, va
 
@@ -821,7 +869,7 @@
 def solution(mesh):
     def local(query, k_cache, v_cache, cache_lens, dest_slot, k_new, v_new):
         dev = lax.axis_index('dp').reshape(1).astype(I32)
-        flat, full = (SLOTS * ROWS, KV, DIM), (SLOTS, ROWS, KV, DIM)
+        flat, full = (SLOTS * ROWS, TILE, DIM), k_cache.shape
         k, v = k_cache.reshape(flat), v_cache.reshape(flat)
         lens = gather_lens(cache_lens)
         pre_send, src = pre_pack(0, True, after(dev, lens), cache_lens, dest_slot, k, v)
@@ -835,8 +883,8 @@
         def fast(args):
             scalars, k, v, pre0, my_lens, query, k_new, v_new, pick = args
             branches = [functools.partial(route, rows) for rows in CLASSES]
-            *came, ko, vo, query, lens_out = lax.switch(pick, branches, (scalars, k, v, pre0, my_lens, query))
-            return *finish(scalars, k, v, came[:2], came[2:], query, k_new, v_new, (ko, vo)), lens_out
+            *post, ko, vo, query, lens_out = lax.switch(pick, branches, (scalars, k, v, pre0, my_lens, query))
+            return *finish(scalars, k, v, post, query, k_new, v_new, (ko, vo)), lens_out
 
         def slow(args):
             (dev, meta, lens, dest, src), k, v, _, _, query, k_new, v_new, _ = args
@@ -844,9 +892,9 @@
             mine = length(lens, lax.dynamic_slice(src, (dev[0] * SLOTS,), (SLOTS,)))
             mine = jnp.tile(jnp.pad(mine, (0, LANES - SLOTS)), DEVS)
             here = (dev, meta, mine, dest, jnp.arange(TOTAL, dtype=I32))
-            none = [jnp.zeros((CHIPS, KV, DIM), BF)] * 2
+            none = [jnp.zeros((CHIPS, TILE, DIM), BF)] * 2
             *outs, lens_out, query = zero_tails(dev, mine, here[-1], query)
-            return *finish(here, ka, va, none, none, query, k_new, v_new, outs), lens_out
+            return *finish(here, ka, va, none, query, k_new, v_new, outs), lens_out
 
         pick = plan[C_ROW, 0]
         attn, ko, vo, lens_out = lax.cond(

time: 242 us -> 231 us (0.955)
  Pallas kernels: 128 us -> 121 us
  waiting for transfers between devices: 76.3 us -> 73.1 us
    pallas_call x1, Pallas kernels: 21.7 us -> 16.9 us  [finish(): local_call(finish_kernel, out_shape=[jax.ShapeDtypeStruct((SLOTS, HEADS,...]
    ppermute x22, waiting for transfers between devices: 76.3 us -> 73.1 us  [swap(): return lax.ppermute(x, 'dp', [(i, i ^ mask) for i in range(DEVS)])]
  transfers between devices with their start and end apart: 22 -> 22, of which waited for: 16 -> 16; matrix products, arithmetic and copies ran while one was open for 0% -> 0% of each run, Pallas kernels for 33% -> 34%
where the time goes in v1:
time: 231 us; the launch traced here: 229 us
  Pallas kernels  121 us (52%)
  waiting for transfers between devices  73.1 us (32%)
  starting transfers between devices  26.2 us (11%)
  local copies, waits for them, and re-layouts  6.09 us (3%)
    ppermute x22, waiting for transfers between devices, swap(): return lax.ppermute(x, 'dp', [(i, i ^ mask) for i in range(DEVS)])  73.1 us
    pallas_call x6, Pallas kernels, pack(): local_call(functools.partial(pack_kernel, beta, step, cap), out_shape=[ro...  35.9 us
    ppermute x22, starting transfers between devices, swap(): return lax.ppermute(x, 'dp', [(i, i ^ mask) for i in range(DEVS)])  26.2 us
    pallas_call x2, Pallas kernels, land(): local_call(functools.partial(post_kernel, beta, False), out_shape=[rows_o...  18.4 us
    pallas_call x1, Pallas kernels, finish(): local_call(finish_kernel, out_shape=[jax.ShapeDtypeStruct((SLOTS, HEADS,...  16.9 us
    pallas_call x2, Pallas kernels, pre_pack(): local_call(functools.partial(pre_kernel, beta, with_src), out_shape=out,...  12 us
    pallas_call x1, Pallas kernels, make_plan(): pl.pallas_call(plan_kernel, out_shape=jax.ShapeDtypeStruct((META_ROWS, LA...  11.2 us
    pallas_call x2, Pallas kernels, post_pack(): local_call(functools.partial(post_kernel, beta, True), out_shape=rows_of(...  10.1 us
  transfers between devices with their start and end apart: 22, of which 16 were waited for; matrix products, arithmetic and copies ran while one was open for 0% of the time, Pallas kernels for 34%

profile of v1, /device:TPU:0, one launch (start us, length us, event | category | flops | bytes accessed | tf_op | source)
XLA Modules:
  0.0 229.0 jit_solution(16267350379495615476)
XLA Ops:
  1.8 8.3 %gather_lens.1 = s32[16,1,128]{2,1,0:T(1,128)S(1)} custom-call(s32[1,128]{1,0:T(1,128)} %pad_bitcast_fusion.x_ref), custom_call_target="tpu_custom_call" | custom-call | tf_op jit(solution)/shard_map/gather_lens/pallas_call | solution.py:236
  10.1 6.5 %shard_map.165 = (bf16[3456,8,128]{2,1,0:T(8,128)(2,1)}, s32[512]{0:T(512)S(1)}) custom-call(s32[1]{0:T(128)} %bitcast.7.dev_ref, s32[32]{0:T(128)} %lens_ref.1, s32[512]{0:T(512)} %dest_ref.1, bf16[8192,8,128]{2,1,0:T(8,128)(2,1)} %bitcast.17, bf16[8192,8,128]{2,1,0:T(8,128)(2,1)} %bitcast.20), custom_call_target="tpu_custom_call" | custom-call | tf_op jit(solution)/shard_map/pallas_call | solution.py:335
  16.7 11.2 %plan.1 = s32[56,128]{1,0:T(8,128)S(1)} custom-call(s32[16,128]{1,0:T(8,128)S(1)} %bitcast.33, s32[4,128]{1,0:T(4,128)S(1)} %bitcast.36, f32[128,128]{1,0:T(8,128)} %constant.119.clone.hop_ref, f32[128,128]{1,0:T(8,128)} %constant.120.clone.hop_t_ref, f32[128,128]{1,0:T(8,128)} %constant.121.clone.group_ref, f32[128,128]{1,0:T(8,128)} %constant.122.clone.before_ref, ...), custom_call_target="tpu_custom_call" | custom-call | tf_op jit(solution)/shard_map/plan/pallas_call | solution.py:210
  29.0 199.2 %conditional.2 = (bf16[32,28,128]{2,1,0:T(8,128)(2,1)S(1)}, bf16[8192,8,128]{2,1,0:T(8,128)(2,1)}, bf16[8192,8,128]{2,1,0:T(8,128)(2,1)}, s32[32]{0:T(128)}) conditional(s32[]{:T(128)} %convert_element_type.3, (s32[]{:T(128)}, s32[512]{0:T(512)S(1)}, s32[2048]{0:T(1024)S(1)}, bf16[8192,8,128]{2,1,0:T(8,128)(2,1)}, bf16[8192,8,128]{2,1,0:T(8,128)(2,1)}, ...), branch_computations={%region_0.3_spmd, %region_3.12_spmd} | conditional | flops 1277 | bytes 369855136 | solution.py:900
  31.4 179.5 %conditional = (bf16[3328,8,128]{2,1,0:T(8,128)(2,1)}, bf16[3328,8,128]{2,1,0:T(8,128)(2,1)}, bf16[8192,8,128]{2,1,0:T(8,128)(2,1)}, bf16[8192,8,128]{2,1,0:T(8,...) conditional(s32[]{:T(128)} %clamp.2, (s32[1]{0:T(128)}, s32[7168]{0:T(1024)}, ...), branch_computations={%region_4.4_spmd, %region_5.5_spmd, %region_6.6_spmd, %region_7.7_... | conditional | bytes 281142784 | solution.py:886
  31.5 5.8 %branch_0_fun.19 = (bf16[544,8,128]{2,1,0:T(8,128)(2,1)}, bf16[544,8,128]{2,1,0:T(8,128)(2,1)}, bf16[544,8,128]{2,1,0:T(8,128)(2,1)}) custom-call(s32[1]{0:T(128)} %get-tuple-element.444.dev_ref, s32[7168]{0:T(1024)} %get-tuple-element.398.meta, s32[2048]{0:T(1024)S(1)} %get-tuple-element.399.lens_ref, s32[512]{0:T(512)} %get-tuple-element.400.dest_ref, ...), custom_call_target="tpu_custom_call" | custom-call | tf_op jit(solution)/shard_map/cond/branch_1_fun/cond/branch_0_fun/pallas_call | solution.py:466
  37.3 5.5 %branch_0_fun.20 = bf16[3456,8,128]{2,1,0:T(8,128)(2,1)} custom-call(s32[1]{0:T(128)} %get-tuple-element.444.dev_ref, s32[32]{0:T(128)S(1)} %copy-done.69, s32[512]{0:T(512)S(1)} %copy-done.27, bf16[8192,8,128]{2,1,0:T(8,128)(2,1)} %get-tuple-element.401.k_ref.rest_4_, bf16[8192,8,128]{2,1,0:T(8,128)(2,1)} %get-tuple-element.402.v_ref.rest_5_), custom_call_target="tpu_custom_call" | custom-call | tf_op jit(solution)/shard_map/cond/branch_1_fun/cond/branch_0_fun/pallas_call | solution.py:335
  42.9 2.5 %collective-permute-start.1 = (bf16[544,8,128]{2,1,0:T(8,128)(2,1)}, bf16[544,8,128]{2,1,0:T(8,128)(2,1)S(1)}, u32[]{:S(2)}, u32[]{:S(2)}) collective-permute-start(bf16[544,8,128]{2,1,0:T(8,128)(2,1)} %get-tuple-element.404), channel_id=1, source_target_pairs={{0,2},{1,3},{2,0},{3,1},{4,6},{5,7},{6,4},{7,5},{8,10},{9,11},{10,... | collective-permute-start | bytes 3342344 | tf_op jit(solution)/shard_map/cond/branch_1_fun/cond/branch_0_fun/ppermute | solution.py:802
  46.7 6.4 %branch_0_fun.21 = (bf16[8192,8,128]{2,1,0:T(8,128)(2,1)}, bf16[8192,8,128]{2,1,0:T(8,128)(2,1)}, s32[32]{0:T(128)}, bf16[32,32,128]{2,1,0:T(8,128)(2,1)}) custom-call(s32[1]{0:T(128)} %get-tuple-element.444.dev_ref, s32[2048]{0:T(1024)S(1)} %get-tuple-element.399.lens_ref, s32[512]{0:T(512)S(1)} %get-tuple-element.408.src_ref, ...), custom_call_target="tpu_custom_call" | custom-call | tf_op jit(solution)/shard_map/cond/branch_1_fun/cond/branch_0_fun/pallas_call | solution.py:652
  53.2 1.8 branch_0_fun.22
  55.0 5.6 %branch_0_fun.23 = (bf16[544,8,128]{2,1,0:T(8,128)(2,1)}, bf16[544,8,128]{2,1,0:T(8,128)(2,1)}, bf16[544,8,128]{2,1,0:T(8,128)(2,1)}) custom-call(s32[1]{0:T(128)} %get-tuple-element.444.dev_ref, s32[7168]{0:T(1024)S(1)} %copy-done.1, s32[2048]{0:T(1024)S(1)} %get-tuple-element.399.lens_ref, s32[512]{0:T(512)S(1)} %copy-done.27, ...), custom_call_target="tpu_custom_call" | custom-call | tf_op jit(solution)/shard_map/cond/branch_1_fun/cond/branch_0_fun/pallas_call | solution.py:466
  60.6 3.9 %collective-permute-start.4 = (bf16[544,8,128]{2,1,0:T(8,128)(2,1)}, bf16[544,8,128]{2,1,0:T(8,128)(2,1)S(1)}, u32[]{:S(2)}, u32[]{:S(2)}) collective-permute-start(bf16[544,8,128]{2,1,0:T(8,128)(2,1)} %get-tuple-element.414), channel_id=1, source_target_pairs={{0,2},{1,3},{2,0},{3,1},{4,6},{5,7},{6,4},{7,5},{8,10},{9,11},{10,... | collective-permute-start | bytes 3342344 | tf_op jit(solution)/shard_map/cond/branch_1_fun/cond/branch_0_fun/ppermute | solution.py:802
  64.4 6.7 %collective-permute-done.1.rest_0_.rest_7_ = bf16[544,8,128]{2,1,0:T(8,128)(2,1)S(1)} collective-permute-done((bf16[544,8,128]{2,1,0:T(8,128)(2,1)}, bf16[544,8,128]{2,1,0:T(8,128)(2,1)S(1)}, u32[]{:S(2)}, u32[]{:S(2)}) %collective-permute-start.1) | collective-permute-done | bytes 1114144 | tf_op jit(solution)/shard_map/cond/branch_1_fun/cond/branch_0_fun/ppermute | solution.py:802
  73.2 5.9 %branch_0_fun.24 = (bf16[544,8,128]{2,1,0:T(8,128)(2,1)}, bf16[544,8,128]{2,1,0:T(8,128)(2,1)}, bf16[544,8,128]{2,1,0:T(8,128)(2,1)}) custom-call(s32[1]{0:T(128)} %get-tuple-element.444.dev_ref, s32[7168]{0:T(1024)S(1)} %copy-done.1, s32[2048]{0:T(1024)S(1)} %get-tuple-element.399.lens_ref, s32[512]{0:T(512)S(1)} %copy-done.27, ...), custom_call_target="tpu_custom_call" | custom-call | tf_op jit(solution)/shard_map/cond/branch_1_fun/cond/branch_0_fun/pallas_call | solution.py:466
  80.8 14.2 %collective-permute-done.4.rest_0_.rest_7_ = bf16[544,8,128]{2,1,0:T(8,128)(2,1)S(1)} collective-permute-done((bf16[544,8,128]{2,1,0:T(8,128)(2,1)}, bf16[544,8,128]{2,1,0:T(8,128)(2,1)S(1)}, u32[]{:S(2)}, u32[]{:S(2)}) %collective-permute-start.4) | collective-permute-done | bytes 1114144 | tf_op jit(solution)/shard_map/cond/branch_1_fun/cond/branch_0_fun/ppermute | solution.py:802
  98.0 6.0 %branch_0_fun.25 = (bf16[544,8,128]{2,1,0:T(8,128)(2,1)}, bf16[544,8,128]{2,1,0:T(8,128)(2,1)}, bf16[544,8,128]{2,1,0:T(8,128)(2,1)}) custom-call(s32[1]{0:T(128)} %get-tuple-element.444.dev_ref, s32[7168]{0:T(1024)S(1)} %copy-done.1, s32[2048]{0:T(1024)S(1)} %get-tuple-element.399.lens_ref, s32[512]{0:T(512)S(1)} %copy-done.27, ...), custom_call_target="tpu_custom_call" | custom-call | tf_op jit(solution)/shard_map/cond/branch_1_fun/cond/branch_0_fun/pallas_call | solution.py:466
  104.0 1.7 collective-permute-start.10
  105.7 13.2 %collective-permute-done.7.rest_3_.rest_10_ = bf16[544,8,128]{2,1,0:T(8,128)(2,1)S(1)} collective-permute-done((bf16[544,8,128]{2,1,0:T(8,128)(2,1)}, bf16[544,8,128]{2,1,0:T(8,128)(2,1)S(1)}, u32[]{:S(2)}, u32[]{:S(2)}) %collective-permute-start.7) | collective-permute-done | bytes 1114144 | tf_op jit(solution)/shard_map/cond/branch_1_fun/cond/branch_0_fun/ppermute | solution.py:802
  121.0 6.3 %branch_0_fun.26 = (bf16[544,8,128]{2,1,0:T(8,128)(2,1)}, bf16[544,8,128]{2,1,0:T(8,128)(2,1)}, bf16[544,8,128]{2,1,0:T(8,128)(2,1)}) custom-call(s32[1]{0:T(128)} %get-tuple-element.444.dev_ref, s32[7168]{0:T(1024)S(1)} %copy-done.1, s32[2048]{0:T(1024)S(1)} %get-tuple-element.399.lens_ref, s32[512]{0:T(512)S(1)} %copy-done.27, ...), custom_call_target="tpu_custom_call" | custom-call | tf_op jit(solution)/shard_map/cond/branch_1_fun/cond/branch_0_fun/pallas_call | solution.py:466
  127.3 1.9 collective-permute-start.13
  129.2 13.5 %collective-permute-done.10.rest_3_.rest_10_ = bf16[544,8,128]{2,1,0:T(8,128)(2,1)S(1)} collective-permute-done((bf16[544,8,128]{2,1,0:T(8,128)(2,1)}, bf16[544,8,128]{2,1,0:T(8,128)(2,1)S(1)}, u32[]{:S(2)}, u32[]{:S(2)}) %collective-permute-start.10) | collective-permute-done | bytes 1114144 | tf_op jit(solution)/shard_map/cond/branch_1_fun/cond/branch_0_fun/ppermute | solution.py:802
  145.8 6.3 %branch_0_fun.27 = (bf16[544,8,128]{2,1,0:T(8,128)(2,1)}, bf16[544,8,128]{2,1,0:T(8,128)(2,1)}, bf16[544,8,128]{2,1,0:T(8,128)(2,1)}) custom-call(s32[1]{0:T(128)} %get-tuple-element.444.dev_ref, s32[7168]{0:T(1024)S(1)} %copy-done.1, s32[2048]{0:T(1024)S(1)} %get-tuple-element.399.lens_ref, s32[512]{0:T(512)S(1)} %copy-done.27, ...), custom_call_target="tpu_custom_call" | custom-call | tf_op jit(solution)/shard_map/cond/branch_1_fun/cond/branch_0_fun/pallas_call | solution.py:466
  152.0 1.6 collective-permute-start.17
  153.7 12.9 %collective-permute-done.13.rest_13_ = bf16[544,8,128]{2,1,0:T(8,128)(2,1)S(1)} collective-permute-done((bf16[544,8,128]{2,1,0:T(8,128)(2,1)}, bf16[544,8,128]{2,1,0:T(8,128)(2,1)S(1)}, u32[]{:S(2)}, u32[]{:S(2)}) %collective-permute-start.13) | collective-permute-done | bytes 1114144 | tf_op jit(solution)/shard_map/cond/branch_1_fun/cond/branch_0_fun/ppermute | solution.py:802
  168.7 5.1 %branch_0_fun.28 = bf16[3328,8,128]{2,1,0:T(8,128)(2,1)} custom-call(s32[1]{0:T(128)} %get-tuple-element.444.dev_ref, s32[7168]{0:T(1024)S(1)} %copy-done.1, s32[2048]{0:T(1024)S(1)} %get-tuple-element.399.lens_ref, s32[512]{0:T(512)S(1)} %copy-done.27, s32[512]{0:T(512)S(1)} %get-tuple-element.408.src_ref, s32[80]{0:T(128)} %get-tuple-element.412.rest_0_, ...), custom_call_target="tpu_custom_call" | custom-call | tf_op jit(solution)/shard_map/cond/branch_1_fun/cond/branch_0_fun/pallas_call | solution.py:600
  173.8 2.5 %collective-permute-start.16 = (bf16[3328,8,128]{2,1,0:T(8,128)(2,1)}, bf16[3328,8,128]{2,1,0:T(8,128)(2,1)}, u32[]{:S(2)}, u32[]{:S(2)}) collective-permute-start(bf16[3328,8,128]{2,1,0:T(8,128)(2,1)} %branch_0_fun.28), channel_id=1, source_target_pairs={{0,1},{1,0},{2,3},{3,2},{4,5},{5,4},{6,7},{7,6},{8,9},{9,8},{10,11... | collective-permute-start | bytes 20447240 | tf_op jit(solution)/shard_map/cond/branch_1_fun/cond/branch_0_fun/ppermute | solution.py:802
  176.3 9.1 %branch_0_fun.29 = (bf16[8192,8,128]{2,1,0:T(8,128)(2,1)}, bf16[8192,8,128]{2,1,0:T(8,128)(2,1)}) custom-call(s32[1]{0:T(128)} %get-tuple-element.444.dev_ref, s32[7168]{0:T(1024)S(1)} %copy-done.1, s32[2048]{0:T(1024)S(1)} %get-tuple-element.399.lens_ref, s32[512]{0:T(512)S(1)} %copy-done.27, ...), custom_call_target="tpu_custom_call", output_to_operand_aliasing={{0}: (21, {}), {1}: (22, {})} | custom-call | tf_op jit(solution)/shard_map/cond/branch_1_fun/cond/branch_0_fun/pallas_call | solution.py:610
  185.5 4.4 %collective-permute-done.17.rest_13_ = bf16[544,8,128]{2,1,0:T(8,128)(2,1)S(1)} collective-permute-done((bf16[544,8,128]{2,1,0:T(8,128)(2,1)}, bf16[544,8,128]{2,1,0:T(8,128)(2,1)S(1)}, u32[]{:S(2)}, u32[]{:S(2)}) %collective-permute-start.17) | collective-permute-done | bytes 1114144 | tf_op jit(solution)/shard_map/cond/branch_1_fun/cond/branch_0_fun/ppermute | solution.py:802
  192.6 5.0 %branch_0_fun.30 = bf16[3328,8,128]{2,1,0:T(8,128)(2,1)} custom-call(s32[1]{0:T(128)} %get-tuple-element.444.dev_ref, s32[7168]{0:T(1024)S(1)} %copy-done.1, s32[2048]{0:T(1024)S(1)} %get-tuple-element.399.lens_ref, s32[512]{0:T(512)S(1)} %copy-done.27, s32[512]{0:T(512)S(1)} %get-tuple-element.408.src_ref, s32[80]{0:T(128)} %get-tuple-element.412.rest_0_, ...), custom_call_target="tpu_custom_call" | custom-call | tf_op jit(solution)/shard_map/cond/branch_1_fun/cond/branch_0_fun/pallas_call | solution.py:600
  197.6 2.5 %collective-permute-start.20 = (bf16[3328,8,128]{2,1,0:T(8,128)(2,1)}, bf16[3328,8,128]{2,1,0:T(8,128)(2,1)}, u32[]{:S(2)}, u32[]{:S(2)}) collective-permute-start(bf16[3328,8,128]{2,1,0:T(8,128)(2,1)} %branch_0_fun.30), channel_id=1, source_target_pairs={{0,1},{1,0},{2,3},{3,2},{4,5},{5,4},{6,7},{7,6},{8,9},{9,8},{10,11... | collective-permute-start | bytes 20447240 | tf_op jit(solution)/shard_map/cond/branch_1_fun/cond/branch_0_fun/ppermute | solution.py:802
  200.1 9.2 %branch_0_fun.31 = (bf16[8192,8,128]{2,1,0:T(8,128)(2,1)}, bf16[8192,8,128]{2,1,0:T(8,128)(2,1)}) custom-call(s32[1]{0:T(128)} %get-tuple-element.444.dev_ref, s32[7168]{0:T(1024)S(1)} %copy-done.1, s32[2048]{0:T(1024)S(1)} %get-tuple-element.399.lens_ref, s32[512]{0:T(512)S(1)} %copy-done.27, ...), custom_call_target="tpu_custom_call", output_to_operand_aliasing={{0}: (21, {}), {1}: (22, {})} | custom-call | tf_op jit(solution)/shard_map/cond/branch_1_fun/cond/branch_0_fun/pallas_call | solution.py:610
  210.9 16.9 %branch_1_fun.27 = (bf16[32,28,128]{2,1,0:T(8,128)(2,1)S(1)}, bf16[8192,8,128]{2,1,0:T(8,128)(2,1)}, bf16[8192,8,128]{2,1,0:T(8,128)(2,1)}) custom-call(s32[1]{0:T(128)} %get-tuple-element.813.dev_ref, s32[2048]{0:T(1024)S(1)} %get-tuple-element.814.lens_ref, s32[512]{0:T(512)S(1)} %get-tuple-element.815.src_ref, ...), custom_call_target="tpu_custom_call", output_to_operand_aliasing={{1}: (10, {}), {2}: (11, {})} | custom-call | tf_op jit(solution)/shard_map/cond/branch_1_fun/pallas_call | solution.py:790
  (71 shorter events, 24.0 us)
Async XLA Ops:
  10.1 6.6 %copy-start.26 = (s32[512]{0:T(512)S(1)}, s32[512]{0:T(512)}, u32[]{:S(2)}) copy-start(s32[512]{0:T(512)} %dest_ref.1) | copy-start | bytes 6148
  10.1 18.9 %copy-start.63 = (bf16[32,28,128]{2,0,1:T(8,128)(2,1)S(1)}, bf16[32,28,128]{2,0,1:T(8,128)(2,1)}, u32[]{:S(2)}) copy-start(bf16[32,28,128]{2,0,1:T(8,128)(2,1)} %param.26) | copy-start | bytes 688132
  16.6 12.4 %collective-permute-start.172 = (bf16[3456,8,128]{2,1,0:T(8,128)(2,1)}, bf16[3456,8,128]{2,1,0:T(8,128)(2,1)}, u32[]{:S(2)}, u32[]{:S(2)}) collective-permute-start(bf16[3456,8,128]{2,1,0:T(8,128)(2,1)} %get-tuple-element.848), channel_id=1, source_target_pairs={{0,1},{1,0},{2,3},{3,2},{4,5},{5,4},{6,7},{7,6},{8,9},{9,8},{10,11... | collective-permute-start | bytes 21233672 | tf_op jit(solution)/shard_map/ppermute | solution.py:802
  31.4 179.5 %copy-start.66 = (bf16[32,4,128]{2,1,0:T(4,128)(2,1)S(1)}, bf16[32,4,128]{2,1,0:T(4,128)(2,1)}, u32[]{:S(2)}) copy-start(bf16[32,4,128]{2,1,0:T(4,128)(2,1)} %get-tuple-element.827.rest_3_) | copy-start | bytes 98308 | tf_op jit(solution)/shard_map/cond
  31.4 179.5 %copy-start.68 = (bf16[32,4,128]{2,1,0:T(4,128)(2,1)S(1)}, bf16[32,4,128]{2,1,0:T(4,128)(2,1)}, u32[]{:S(2)}) copy-start(bf16[32,4,128]{2,1,0:T(4,128)(2,1)} %get-tuple-element.828.rest_4_) | copy-start | bytes 98308 | tf_op jit(solution)/shard_map/cond
  31.5 5.9 %copy-start.27 = (s32[512]{0:T(512)S(1)}, s32[512]{0:T(512)}, u32[]{:S(2)}) copy-start(s32[512]{0:T(512)} %get-tuple-element.400.dest_ref) | copy-start | bytes 6148 | tf_op jit(solution)/shard_map/cond/branch_1_fun/cond
  31.5 5.9 %copy-start.69 = (s32[32]{0:T(128)S(1)}, s32[32]{0:T(128)}, u32[]{:S(2)}) copy-start(s32[32]{0:T(128)} %get-tuple-element.406.lens_ref) | copy-start | bytes 388 | tf_op jit(solution)/shard_map/cond/branch_1_fun/cond
  37.3 15.9 %copy-start.1 = (s32[7168]{0:T(1024)S(1)}, s32[7168]{0:T(1024)}, u32[]{:S(2)}) copy-start(s32[7168]{0:T(1024)} %get-tuple-element.398.meta) | copy-start | bytes 86020 | tf_op jit(solution)/shard_map/cond/branch_1_fun/cond
  42.9 12.1 %collective-permute-start = (bf16[3456,8,128]{2,1,0:T(8,128)(2,1)}, bf16[3456,8,128]{2,1,0:T(8,128)(2,1)}, u32[]{:S(2)}, u32[]{:S(2)}) collective-permute-start(bf16[3456,8,128]{2,1,0:T(8,128)(2,1)} %branch_0_fun.20), channel_id=1, source_target_pairs={{0,1},{1,0},{2,3},{3,2},{4,5},{5,4},{6,7},{7,6},{8,9},{9,8},{10,11... | collective-permute-start | bytes 21233672 | tf_op jit(solution)/shard_map/cond/branch_1_fun/cond/branch_0_fun/ppermute | solution.py:802
  42.9 28.2 %collective-permute-start.1 = (bf16[544,8,128]{2,1,0:T(8,128)(2,1)}, bf16[544,8,128]{2,1,0:T(8,128)(2,1)S(1)}, u32[]{:S(2)}, u32[]{:S(2)}) collective-permute-start(bf16[544,8,128]{2,1,0:T(8,128)(2,1)} %get-tuple-element.404), channel_id=1, source_target_pairs={{0,2},{1,3},{2,0},{3,1},{4,6},{5,7},{6,4},{7,5},{8,10},{9,11},{10,... | collective-permute-start | bytes 3342344 | tf_op jit(solution)/shard_map/cond/branch_1_fun/cond/branch_0_fun/ppermute | solution.py:802
  45.5 27.8 %collective-permute-start.2 = (bf16[544,8,128]{2,1,0:T(8,128)(2,1)}, bf16[544,8,128]{2,1,0:T(8,128)(2,1)}, u32[]{:S(2)}, u32[]{:S(2)}) collective-permute-start(bf16[544,8,128]{2,1,0:T(8,128)(2,1)} %get-tuple-element.416), channel_id=1, source_target_pairs={{0,4},{1,5},{2,6},{3,7},{4,0},{5,1},{6,2},{7,3},{8,12},{9,13},{10,... | collective-permute-start | bytes 3342344 | tf_op jit(solution)/shard_map/cond/branch_1_fun/cond/branch_0_fun/ppermute | solution.py:802
  45.5 27.8 %collective-permute-start.3 = (bf16[544,8,128]{2,1,0:T(8,128)(2,1)}, bf16[544,8,128]{2,1,0:T(8,128)(2,1)}, u32[]{:S(2)}, u32[]{:S(2)}) collective-permute-start(bf16[544,8,128]{2,1,0:T(8,128)(2,1)} %get-tuple-element.417), channel_id=1, source_target_pairs={{0,8},{1,9},{2,10},{3,11},{4,12},{5,13},{6,14},{7,15},{8,0},{9,1},... | collective-permute-start | bytes 3342344 | tf_op jit(solution)/shard_map/cond/branch_1_fun/cond/branch_0_fun/ppermute | solution.py:802
  60.6 34.4 %collective-permute-start.4 = (bf16[544,8,128]{2,1,0:T(8,128)(2,1)}, bf16[544,8,128]{2,1,0:T(8,128)(2,1)S(1)}, u32[]{:S(2)}, u32[]{:S(2)}) collective-permute-start(bf16[544,8,128]{2,1,0:T(8,128)(2,1)} %get-tuple-element.414), channel_id=1, source_target_pairs={{0,2},{1,3},{2,0},{3,1},{4,6},{5,7},{6,4},{7,5},{8,10},{9,11},{10,... | collective-permute-start | bytes 3342344 | tf_op jit(solution)/shard_map/cond/branch_1_fun/cond/branch_0_fun/ppermute | solution.py:802
  64.4 32.6 %collective-permute-start.5 = (bf16[544,8,128]{2,1,0:T(8,128)(2,1)}, bf16[544,8,128]{2,1,0:T(8,128)(2,1)S(1)}, u32[]{:S(2)}, u32[]{:S(2)}) collective-permute-start(bf16[544,8,128]{2,1,0:T(8,128)(2,1)} %get-tuple-element.420), channel_id=1, source_target_pairs={{0,4},{1,5},{2,6},{3,7},{4,0},{5,1},{6,2},{7,3},{8,12},{9,13},{10,... | collective-permute-start | bytes 3342344 | tf_op jit(solution)/shard_map/cond/branch_1_fun/cond/branch_0_fun/ppermute | solution.py:802
  71.1 2.1 copy-start.24
  71.1 26.0 %collective-permute-start.6 = (bf16[544,8,128]{2,1,0:T(8,128)(2,1)}, bf16[544,8,128]{2,1,0:T(8,128)(2,1)}, u32[]{:S(2)}, u32[]{:S(2)}) collective-permute-start(bf16[544,8,128]{2,1,0:T(8,128)(2,1)} %get-tuple-element.421), channel_id=1, source_target_pairs={{0,8},{1,9},{2,10},{3,11},{4,12},{5,13},{6,14},{7,15},{8,0},{9,1},... | collective-permute-start | bytes 3342344 | tf_op jit(solution)/shard_map/cond/branch_1_fun/cond/branch_0_fun/ppermute | solution.py:802
  79.2 39.7 %collective-permute-start.7 = (bf16[544,8,128]{2,1,0:T(8,128)(2,1)}, bf16[544,8,128]{2,1,0:T(8,128)(2,1)S(1)}, u32[]{:S(2)}, u32[]{:S(2)}) collective-permute-start(bf16[544,8,128]{2,1,0:T(8,128)(2,1)} %get-tuple-element.418), channel_id=1, source_target_pairs={{0,2},{1,3},{2,0},{3,1},{4,6},{5,7},{6,4},{7,5},{8,10},{9,11},{10,... | collective-permute-start | bytes 3342344 | tf_op jit(solution)/shard_map/cond/branch_1_fun/cond/branch_0_fun/ppermute | solution.py:802
  80.8 40.2 %collective-permute-start.8 = (bf16[544,8,128]{2,1,0:T(8,128)(2,1)}, bf16[544,8,128]{2,1,0:T(8,128)(2,1)}, u32[]{:S(2)}, u32[]{:S(2)}) collective-permute-start(bf16[544,8,128]{2,1,0:T(8,128)(2,1)} %get-tuple-element.424), channel_id=1, source_target_pairs={{0,4},{1,5},{2,6},{3,7},{4,0},{5,1},{6,2},{7,3},{8,12},{9,13},{10,... | collective-permute-start | bytes 3342344 | tf_op jit(solution)/shard_map/cond/branch_1_fun/cond/branch_0_fun/ppermute | solution.py:802
  95.0 26.0 %collective-permute-start.9 = (bf16[544,8,128]{2,1,0:T(8,128)(2,1)}, bf16[544,8,128]{2,1,0:T(8,128)(2,1)}, u32[]{:S(2)}, u32[]{:S(2)}) collective-permute-start(bf16[544,8,128]{2,1,0:T(8,128)(2,1)} %get-tuple-element.425), channel_id=1, source_target_pairs={{0,8},{1,9},{2,10},{3,11},{4,12},{5,13},{6,14},{7,15},{8,0},{9,1},... | collective-permute-start | bytes 3342344 | tf_op jit(solution)/shard_map/cond/branch_1_fun/cond/branch_0_fun/ppermute | solution.py:802
  104.0 38.8 %collective-permute-start.10 = (bf16[544,8,128]{2,1,0:T(8,128)(2,1)}, bf16[544,8,128]{2,1,0:T(8,128)(2,1)S(1)}, u32[]{:S(2)}, u32[]{:S(2)}) collective-permute-start(bf16[544,8,128]{2,1,0:T(8,128)(2,1)} %get-tuple-element.422), channel_id=1, source_target_pairs={{0,2},{1,3},{2,0},{3,1},{4,6},{5,7},{6,4},{7,5},{8,10},{9,11},{10,... | collective-permute-start | bytes 3342344 | tf_op jit(solution)/shard_map/cond/branch_1_fun/cond/branch_0_fun/ppermute | solution.py:802
  105.7 39.1 %collective-permute-start.11 = (bf16[544,8,128]{2,1,0:T(8,128)(2,1)}, bf16[544,8,128]{2,1,0:T(8,128)(2,1)S(1)}, u32[]{:S(2)}, u32[]{:S(2)}) collective-permute-start(bf16[544,8,128]{2,1,0:T(8,128)(2,1)} %get-tuple-element.428), channel_id=1, source_target_pairs={{0,4},{1,5},{2,6},{3,7},{4,0},{5,1},{6,2},{7,3},{8,12},{9,13},{10,... | collective-permute-start | bytes 3342344 | tf_op jit(solution)/shard_map/cond/branch_1_fun/cond/branch_0_fun/ppermute | solution.py:802
  118.9 2.1 copy-start.47
  118.9 26.0 %collective-permute-start.12 = (bf16[544,8,128]{2,1,0:T(8,128)(2,1)}, bf16[544,8,128]{2,1,0:T(8,128)(2,1)}, u32[]{:S(2)}, u32[]{:S(2)}) collective-permute-start(bf16[544,8,128]{2,1,0:T(8,128)(2,1)} %get-tuple-element.429), channel_id=1, source_target_pairs={{0,8},{1,9},{2,10},{3,11},{4,12},{5,13},{6,14},{7,15},{8,0},{9,1},... | collective-permute-start | bytes 3342344 | tf_op jit(solution)/shard_map/cond/branch_1_fun/cond/branch_0_fun/ppermute | solution.py:802
  127.3 39.3 %collective-permute-start.13 = (bf16[544,8,128]{2,1,0:T(8,128)(2,1)}, bf16[544,8,128]{2,1,0:T(8,128)(2,1)S(1)}, u32[]{:S(2)}, u32[]{:S(2)}) collective-permute-start(bf16[544,8,128]{2,1,0:T(8,128)(2,1)} %get-tuple-element.426), channel_id=1, source_target_pairs={{0,2},{1,3},{2,0},{3,1},{4,6},{5,7},{6,4},{7,5},{8,10},{9,11},{10,... | collective-permute-start | bytes 3342344 | tf_op jit(solution)/shard_map/cond/branch_1_fun/cond/branch_0_fun/ppermute | solution.py:802
  129.2 39.5 %collective-permute-start.14 = (bf16[544,8,128]{2,1,0:T(8,128)(2,1)}, bf16[544,8,128]{2,1,0:T(8,128)(2,1)}, u32[]{:S(2)}, u32[]{:S(2)}) collective-permute-start(bf16[544,8,128]{2,1,0:T(8,128)(2,1)} %get-tuple-element.435), channel_id=1, source_target_pairs={{0,4},{1,5},{2,6},{3,7},{4,0},{5,1},{6,2},{7,3},{8,12},{9,13},{10,... | collective-permute-start | bytes 3342344 | tf_op jit(solution)/shard_map/cond/branch_1_fun/cond/branch_0_fun/ppermute | solution.py:802
  142.7 26.0 %collective-permute-start.15 = (bf16[544,8,128]{2,1,0:T(8,128)(2,1)}, bf16[544,8,128]{2,1,0:T(8,128)(2,1)}, u32[]{:S(2)}, u32[]{:S(2)}) collective-permute-start(bf16[544,8,128]{2,1,0:T(8,128)(2,1)} %get-tuple-element.436), channel_id=1, source_target_pairs={{0,8},{1,9},{2,10},{3,11},{4,12},{5,13},{6,14},{7,15},{8,0},{9,1},... | collective-permute-start | bytes 3342344 | tf_op jit(solution)/shard_map/cond/branch_1_fun/cond/branch_0_fun/ppermute | solution.py:802
  152.0 37.8 %collective-permute-start.17 = (bf16[544,8,128]{2,1,0:T(8,128)(2,1)}, bf16[544,8,128]{2,1,0:T(8,128)(2,1)S(1)}, u32[]{:S(2)}, u32[]{:S(2)}) collective-permute-start(bf16[544,8,128]{2,1,0:T(8,128)(2,1)} %get-tuple-element.430), channel_id=1, source_target_pairs={{0,2},{1,3},{2,0},{3,1},{4,6},{5,7},{6,4},{7,5},{8,10},{9,11},{10,... | collective-permute-start | bytes 3342344 | tf_op jit(solution)/shard_map/cond/branch_1_fun/cond/branch_0_fun/ppermute | solution.py:802
  153.7 37.6 %collective-permute-start.18 = (bf16[544,8,128]{2,1,0:T(8,128)(2,1)}, bf16[544,8,128]{2,1,0:T(8,128)(2,1)S(1)}, u32[]{:S(2)}, u32[]{:S(2)}) collective-permute-start(bf16[544,8,128]{2,1,0:T(8,128)(2,1)} %get-tuple-element.442), channel_id=1, source_target_pairs={{0,4},{1,5},{2,6},{3,7},{4,0},{5,1},{6,2},{7,3},{8,12},{9,13},{10,... | collective-permute-start | bytes 3342344 | tf_op jit(solution)/shard_map/cond/branch_1_fun/cond/branch_0_fun/ppermute | solution.py:802
  166.6 26.0 %collective-permute-start.19 = (bf16[544,8,128]{2,1,0:T(8,128)(2,1)}, bf16[544,8,128]{2,1,0:T(8,128)(2,1)}, u32[]{:S(2)}, u32[]{:S(2)}) collective-permute-start(bf16[544,8,128]{2,1,0:T(8,128)(2,1)} %get-tuple-element.443), channel_id=1, source_target_pairs={{0,8},{1,9},{2,10},{3,11},{4,12},{5,13},{6,14},{7,15},{8,0},{9,1},... | collective-permute-start | bytes 3342344 | tf_op jit(solution)/shard_map/cond/branch_1_fun/cond/branch_0_fun/ppermute | solution.py:802
  173.8 35.5 %collective-permute-start.16 = (bf16[3328,8,128]{2,1,0:T(8,128)(2,1)}, bf16[3328,8,128]{2,1,0:T(8,128)(2,1)}, u32[]{:S(2)}, u32[]{:S(2)}) collective-permute-start(bf16[3328,8,128]{2,1,0:T(8,128)(2,1)} %branch_0_fun.28), channel_id=1, source_target_pairs={{0,1},{1,0},{2,3},{3,2},{4,5},{5,4},{6,7},{7,6},{8,9},{9,8},{10,11... | collective-permute-start | bytes 20447240 | tf_op jit(solution)/shard_map/cond/branch_1_fun/cond/branch_0_fun/ppermute | solution.py:802
  189.8 2.7 %copy-start.60 = (bf16[544,8,128]{2,1,0:T(8,128)(2,1)}, bf16[544,8,128]{2,1,0:T(8,128)(2,1)S(1)}, u32[]{:S(2)}) copy-start(bf16[544,8,128]{2,1,0:T(8,128)(2,1)S(1)} %collective-permute-done.17.rest_13_) | copy-start | bytes 3342340 | tf_op jit(solution)/shard_map/cond/branch_1_fun/cond
  197.6 13.3 %collective-permute-start.20 = (bf16[3328,8,128]{2,1,0:T(8,128)(2,1)}, bf16[3328,8,128]{2,1,0:T(8,128)(2,1)}, u32[]{:S(2)}, u32[]{:S(2)}) collective-permute-start(bf16[3328,8,128]{2,1,0:T(8,128)(2,1)} %branch_0_fun.30), channel_id=1, source_target_pairs={{0,1},{1,0},{2,3},{3,2},{4,5},{5,4},{6,7},{7,6},{8,9},{9,8},{10,11... | collective-permute-start | bytes 20447240 | tf_op jit(solution)/shard_map/cond/branch_1_fun/cond/branch_0_fun/ppermute | solution.py:802
  (8 other events, 11.5 us)

commit v2 on v1

--- a/solution.py
+++ b/solution.py
@@ -22,7 +22,7 @@
 PRE = 3456
 POST = 3328
 HALF = ROWS // 2
-CLASSES = (1088, 1208, 1312, 1424, 1552, 1648, 1816, 2304)
+CLASSES = (1080, 1200, 1304, 1408, 1528, 1648, 1840, 2400)
 ITERS, FIRST_STEP, SHRINK, MOMENTUM = 10, 0.675, 0.838, 0.9
 LAST = jnp.iinfo(jnp.int32).max
 VMEM_LIMIT = 62914560
@@ -82,10 +82,10 @@
     group = np.zeros_like(hop)
     before = np.zeros_like(hop)
     dest = np.zeros((CHIPS, LANES), np.float32)
-    first = np.zeros_like(dest)
+    last = np.zeros_like(dest)
     for o, (b, hops) in enumerate(OPTIONS):
         dest[b, o] = 1
-        first[:, o] = o == OPT_BASE[b - 1]
+        last[:, o] = o == OPT_BASE[b - 1] + OPT_COUNT[b - 1] - 1
         for step, place, k in hops:
             hop[o, place * PLACE_LANES + step * 3 + k] = 1
         for q, (bb, _) in enumerate(OPTIONS):
@@ -93,10 +93,10 @@
                 group[o, q] = 1
                 before[o, q] = o < q
     tri = np.triu(np.ones_like(hop), 1)
-    return hop, hop.T.copy(), group, before, dest, first, tri
-
-
-def plan_kernel(lens_ref, dest_ref, hop_ref, hop_t_ref, group_ref, before_ref, dmat_ref, first_ref, tri_ref, out_ref):
+    return hop, hop.T.copy(), group, before, dest, last, tri
+
+
+def plan_kernel(lens_ref, dest_ref, hop_ref, hop_t_ref, group_ref, before_ref, dmat_ref, last_ref, tri_ref, out_ref):
     exact = functools.partial(jnp.dot, preferred_element_type=F32, precision=lax.Precision.HIGHEST)
 
     def plain(a, b):
@@ -177,11 +177,13 @@
     start = (weight, weight, 3e38 * one, jnp.zeros(shape, F32), FIRST_STEP * one)
     best = lax.fori_loop(0, ITERS, improve, start)[1]
 
+    best = best / jnp.where(used, exact(best, group_ref[...]), 1.0)
+    begins = exact(best, before_ref[...])
     pick = jnp.zeros((1, 1), I32)
     for t in range(2):
         total = demand[t]
-        x = jnp.minimum(jnp.floor(best * total * 0.995), total)
-        x = x + first_ref[...] * (total - exact(x, group_ref[...]))
+        lo = jnp.floor(total * begins)
+        x = jnp.where(last_ref[...] > 0, total, pltpu.roll(lo, LANES - 1, 1)) - lo
         top = top_of(link_loads(x, exact))
         top = jnp.where(top_of(-x) > 0.0, 1e6, top)
         need = jnp.zeros((1, 1), I32)
@@ -191,7 +193,7 @@
         at = X_ROW + CHIPS * t
         out_ref[at:at + CHIPS, :] = x.astype(I32)
         at = LO_ROW + CHIPS * t
-        out_ref[at:at + CHIPS, :] = exact(x, before_ref[...]).astype(I32)
+        out_ref[at:at + CHIPS, :] = lo.astype(I32)
 
     from_dev = 2 * row + (lane >> 5)
     to_dev = to >> 5
@@ -816,7 +818,8 @@
             if step == 0 and beta == 1:
                 pre_send = pre_pack(1, False, turn, my_lens, dest, k, v)
                 pre[1] = swap(pre_send, 1)
-                ko, vo, lens_out, query = zero_tails(after(dev, pre_send), lens, src, query)
+                ko, vo, lens_out, query = zero_tails(
+                    after(dev, pre_send), lens, src, after(query, pre_send).transpose(1, 0, 2))
                 tables = arrivals(after(dev, lens_out), meta)
                 turn = after(dev, tables[0])
             sends = pack(beta, step, cap, (turn, *scalars[1:]), k, v, pre[beta], recv[beta])
@@ -893,12 +896,13 @@
             mine = jnp.tile(jnp.pad(mine, (0, LANES - SLOTS)), DEVS)
             here = (dev, meta, mine, dest, jnp.arange(TOTAL, dtype=I32))
             none = [jnp.zeros((CHIPS, TILE, DIM), BF)] * 2
-            *outs, lens_out, query = zero_tails(dev, mine, here[-1], query)
+            *outs, lens_out, query = zero_tails(dev, mine, here[-1], after(query, ka).transpose(1, 0, 2))
             return *finish(here, ka, va, none, query, k_new, v_new, outs), lens_out
 
         pick = plan[C_ROW, 0]
         attn, ko, vo, lens_out = lax.cond(
-            pick < len(CLASSES), fast, slow, (scalars, k, v, pre0, cache_lens, query, k_new, v_new, pick))
+            pick < len(CLASSES), fast, slow,
+            (scalars, k, v, pre0, cache_lens, query.transpose(1, 0, 2), k_new, v_new, pick))
         return attn, ko.reshape(full), vo.reshape(full), lens_out
 
     row_spec = P('dp')

time: 231 us -> 229 us (level)
  transfers between devices with their start and end apart: 22 -> 22, of which waited for: 16 -> 14; matrix products, arithmetic and copies ran while one was open for 0% -> 1% of each run, Pallas kernels for 34% -> 34%
where the time goes in v2:
time: 229 us; the launch traced here: 227 us
  Pallas kernels  121 us (53%)
  waiting for transfers between devices  71.8 us (31%)
  starting transfers between devices  26.3 us (11%)
  local copies, waits for them, and re-layouts  5.31 us (2%)
    ppermute x22, waiting for transfers between devices, swap(): return lax.ppermute(x, 'dp', [(i, i ^ mask) for i in range(DEVS)])  71.8 us
    pallas_call x6, Pallas kernels, pack(): local_call(functools.partial(pack_kernel, beta, step, cap), out_shape=[ro...  35.9 us
    ppermute x22, starting transfers between devices, swap(): return lax.ppermute(x, 'dp', [(i, i ^ mask) for i in range(DEVS)])  26.3 us
    pallas_call x2, Pallas kernels, land(): local_call(functools.partial(post_kernel, beta, False), out_shape=[rows_o...  18.5 us
    pallas_call x1, Pallas kernels, finish(): local_call(finish_kernel, out_shape=[jax.ShapeDtypeStruct((SLOTS, HEADS,...  16.9 us
    pallas_call x2, Pallas kernels, pre_pack(): local_call(functools.partial(pre_kernel, beta, with_src), out_shape=out,...  12 us
    pallas_call x1, Pallas kernels, make_plan(): pl.pallas_call(plan_kernel, out_shape=jax.ShapeDtypeStruct((META_ROWS, LA...  11.1 us
    pallas_call x2, Pallas kernels, post_pack(): local_call(functools.partial(post_kernel, beta, True), out_shape=rows_of(...  10.1 us
  transfers between devices with their start and end apart: 22, of which 14 were waited for; matrix products, arithmetic and copies ran while one was open for 1% of the time, Pallas kernels for 34%

profile of v2, /device:TPU:0, one launch (start us, length us, event | category | flops | bytes accessed | tf_op | source)
XLA Modules:
  0.0 227.0 jit_solution(13428662021858807515)
XLA Ops:
  1.8 8.3 %gather_lens.1 = s32[16,1,128]{2,1,0:T(1,128)S(1)} custom-call(s32[1,128]{1,0:T(1,128)} %pad_bitcast_fusion.x_ref), custom_call_target="tpu_custom_call" | custom-call | tf_op jit(solution)/shard_map/gather_lens/pallas_call | solution.py:238
  10.1 6.5 %shard_map.165 = (bf16[3456,8,128]{2,1,0:T(8,128)(2,1)}, s32[512]{0:T(512)S(1)}) custom-call(s32[1]{0:T(128)} %bitcast.16.dev_ref, s32[32]{0:T(128)} %lens_ref.1, s32[512]{0:T(512)} %dest_ref.1, bf16[8192,8,128]{2,1,0:T(8,128)(2,1)} %bitcast.29, bf16[8192,8,128]{2,1,0:T(8,128)(2,1)} %bitcast.32), custom_call_target="tpu_custom_call" | custom-call | tf_op jit(solution)/shard_map/pallas_call | solution.py:337
  16.7 11.1 %plan.1 = s32[56,128]{1,0:T(8,128)S(1)} custom-call(s32[16,128]{1,0:T(8,128)S(1)} %bitcast.45, s32[4,128]{1,0:T(4,128)S(1)} %bitcast.59, f32[128,128]{1,0:T(8,128)} %constant.119.clone.hop_ref, f32[128,128]{1,0:T(8,128)} %constant.120.clone.hop_t_ref, f32[128,128]{1,0:T(8,128)} %constant.121.clone.group_ref, f32[128,128]{1,0:T(8,128)} %constant.122.clone.before_ref, ...), custom_call_target="tpu_custom_call" | custom-call | tf_op jit(solution)/shard_map/plan/pallas_call | solution.py:212
  29.8 196.3 %conditional.2 = (bf16[32,28,128]{2,1,0:T(8,128)(2,1)S(1)}, bf16[8192,8,128]{2,1,0:T(8,128)(2,1)}, bf16[8192,8,128]{2,1,0:T(8,128)(2,1)}, s32[32]{0:T(128)}) conditional(s32[]{:T(128)} %convert_element_type.3, (s32[]{:T(128)}, s32[512]{0:T(512)S(1)}, s32[2048]{0:T(1024)S(1)}, bf16[8192,8,128]{2,1,0:T(8,128)(2,1)}, bf16[8192,8,128]{2,1,0:T(8,128)(2,1)}, ...), branch_computations={%region_0.3_spmd, %region_3.12_spmd} | conditional | flops 1277 | bytes 370313920 | solution.py:903
  30.5 178.4 %conditional = (bf16[3328,8,128]{2,1,0:T(8,128)(2,1)}, bf16[3328,8,128]{2,1,0:T(8,128)(2,1)}, bf16[8192,8,128]{2,1,0:T(8,128)(2,1)}, bf16[8192,8,128]{2,1,0:T(8,...) conditional(s32[]{:T(128)} %clamp.2, (s32[1]{0:T(128)}, s32[7168]{0:T(1024)}, ...), branch_computations={%region_4.4_spmd, %region_5.5_spmd, %region_6.6_spmd, %region_7.7_... | conditional | bytes 290317824 | solution.py:889
  30.6 5.8 %branch_0_fun.19 = (bf16[540,8,128]{2,1,0:T(8,128)(2,1)}, bf16[540,8,128]{2,1,0:T(8,128)(2,1)}, bf16[540,8,128]{2,1,0:T(8,128)(2,1)}) custom-call(s32[1]{0:T(128)} %get-tuple-element.446.dev_ref, s32[7168]{0:T(1024)} %get-tuple-element.399.meta, s32[2048]{0:T(1024)S(1)} %get-tuple-element.400.lens_ref, s32[512]{0:T(512)} %get-tuple-element.401.dest_ref, ...), custom_call_target="tpu_custom_call" | custom-call | tf_op jit(solution)/shard_map/cond/branch_1_fun/cond/branch_0_fun/pallas_call | solution.py:468
  36.4 5.5 %branch_0_fun.20 = bf16[3456,8,128]{2,1,0:T(8,128)(2,1)} custom-call(s32[1]{0:T(128)} %get-tuple-element.446.dev_ref, s32[32]{0:T(128)S(1)} %copy-done.77, s32[512]{0:T(512)S(1)} %copy-done.36, bf16[8192,8,128]{2,1,0:T(8,128)(2,1)} %get-tuple-element.402.k_ref.rest_4_, bf16[8192,8,128]{2,1,0:T(8,128)(2,1)} %get-tuple-element.403.v_ref.rest_5_), custom_call_target="tpu_custom_call" | custom-call | tf_op jit(solution)/shard_map/cond/branch_1_fun/cond/branch_0_fun/pallas_call | solution.py:337
  41.9 2.6 %collective-permute-start.1 = (bf16[540,8,128]{2,1,0:T(8,128)(2,1)}, bf16[540,8,128]{2,1,0:T(8,128)(2,1)S(1)}, u32[]{:S(2)}, u32[]{:S(2)}) collective-permute-start(bf16[540,8,128]{2,1,0:T(8,128)(2,1)} %get-tuple-element.405), channel_id=1, source_target_pairs={{0,2},{1,3},{2,0},{3,1},{4,6},{5,7},{6,4},{7,5},{8,10},{9,11},{10,... | collective-permute-start | bytes 3317768 | tf_op jit(solution)/shard_map/cond/branch_1_fun/cond/branch_0_fun/ppermute | solution.py:804
  45.7 6.4 %branch_0_fun.21 = (bf16[8192,8,128]{2,1,0:T(8,128)(2,1)}, bf16[8192,8,128]{2,1,0:T(8,128)(2,1)}, s32[32]{0:T(128)}, bf16[32,32,128]{2,1,0:T(8,128)(2,1)}) custom-call(s32[1]{0:T(128)} %get-tuple-element.446.dev_ref, s32[2048]{0:T(1024)S(1)} %get-tuple-element.400.lens_ref, s32[512]{0:T(512)S(1)} %get-tuple-element.409.src_ref, bf16[32,28,128]{2,1,0:T(8,128)(2,1)S(1)} %bitcast.51), custom_call_target="tpu_custom_call" | custom-call | tf_op jit(solution)/shard_map/cond/branch_1_fun/cond/branch_0_fun/pallas_call | solution.py:654
  52.2 1.8 branch_0_fun.22
  54.0 5.6 %branch_0_fun.23 = (bf16[540,8,128]{2,1,0:T(8,128)(2,1)}, bf16[540,8,128]{2,1,0:T(8,128)(2,1)}, bf16[540,8,128]{2,1,0:T(8,128)(2,1)}) custom-call(s32[1]{0:T(128)} %get-tuple-element.446.dev_ref, s32[7168]{0:T(1024)S(1)} %copy-done.1, s32[2048]{0:T(1024)S(1)} %get-tuple-element.400.lens_ref, s32[512]{0:T(512)S(1)} %copy-done.36, ...), custom_call_target="tpu_custom_call" | custom-call | tf_op jit(solution)/shard_map/cond/branch_1_fun/cond/branch_0_fun/pallas_call | solution.py:468
  59.6 3.8 %collective-permute-start.4 = (bf16[540,8,128]{2,1,0:T(8,128)(2,1)}, bf16[540,8,128]{2,1,0:T(8,128)(2,1)S(1)}, u32[]{:S(2)}, u32[]{:S(2)}) collective-permute-start(bf16[540,8,128]{2,1,0:T(8,128)(2,1)} %get-tuple-element.416), channel_id=1, source_target_pairs={{0,2},{1,3},{2,0},{3,1},{4,6},{5,7},{6,4},{7,5},{8,10},{9,11},{10,... | collective-permute-start | bytes 3317768 | tf_op jit(solution)/shard_map/cond/branch_1_fun/cond/branch_0_fun/ppermute | solution.py:804
  63.5 6.5 %collective-permute-done.1.rest_0_.rest_7_ = bf16[540,8,128]{2,1,0:T(8,128)(2,1)S(1)} collective-permute-done((bf16[540,8,128]{2,1,0:T(8,128)(2,1)}, bf16[540,8,128]{2,1,0:T(8,128)(2,1)S(1)}, u32[]{:S(2)}, u32[]{:S(2)}) %collective-permute-start.1) | collective-permute-done | bytes 1105952 | tf_op jit(solution)/shard_map/cond/branch_1_fun/cond/branch_0_fun/ppermute | solution.py:804
  72.1 5.9 %branch_0_fun.24 = (bf16[540,8,128]{2,1,0:T(8,128)(2,1)}, bf16[540,8,128]{2,1,0:T(8,128)(2,1)}, bf16[540,8,128]{2,1,0:T(8,128)(2,1)}) custom-call(s32[1]{0:T(128)} %get-tuple-element.446.dev_ref, s32[7168]{0:T(1024)S(1)} %copy-done.1, s32[2048]{0:T(1024)S(1)} %get-tuple-element.400.lens_ref, s32[512]{0:T(512)S(1)} %copy-done.36, ...), custom_call_target="tpu_custom_call" | custom-call | tf_op jit(solution)/shard_map/cond/branch_1_fun/cond/branch_0_fun/pallas_call | solution.py:468
  79.6 14.0 %collective-permute-done.4.rest_0_.rest_7_ = bf16[540,8,128]{2,1,0:T(8,128)(2,1)S(1)} collective-permute-done((bf16[540,8,128]{2,1,0:T(8,128)(2,1)}, bf16[540,8,128]{2,1,0:T(8,128)(2,1)S(1)}, u32[]{:S(2)}, u32[]{:S(2)}) %collective-permute-start.4) | collective-permute-done | bytes 1105952 | tf_op jit(solution)/shard_map/cond/branch_1_fun/cond/branch_0_fun/ppermute | solution.py:804
  96.7 6.0 %branch_0_fun.25 = (bf16[540,8,128]{2,1,0:T(8,128)(2,1)}, bf16[540,8,128]{2,1,0:T(8,128)(2,1)}, bf16[540,8,128]{2,1,0:T(8,128)(2,1)}) custom-call(s32[1]{0:T(128)} %get-tuple-element.446.dev_ref, s32[7168]{0:T(1024)S(1)} %copy-done.1, s32[2048]{0:T(1024)S(1)} %get-tuple-element.400.lens_ref, s32[512]{0:T(512)S(1)} %copy-done.36, ...), custom_call_target="tpu_custom_call" | custom-call | tf_op jit(solution)/shard_map/cond/branch_1_fun/cond/branch_0_fun/pallas_call | solution.py:468
  102.7 1.7 collective-permute-start.10
  104.4 13.0 %collective-permute-done.7.rest_3_.rest_10_ = bf16[540,8,128]{2,1,0:T(8,128)(2,1)S(1)} collective-permute-done((bf16[540,8,128]{2,1,0:T(8,128)(2,1)}, bf16[540,8,128]{2,1,0:T(8,128)(2,1)S(1)}, u32[]{:S(2)}, u32[]{:S(2)}) %collective-permute-start.7) | collective-permute-done | bytes 1105952 | tf_op jit(solution)/shard_map/cond/branch_1_fun/cond/branch_0_fun/ppermute | solution.py:804
  119.5 6.4 %branch_0_fun.26 = (bf16[540,8,128]{2,1,0:T(8,128)(2,1)}, bf16[540,8,128]{2,1,0:T(8,128)(2,1)}, bf16[540,8,128]{2,1,0:T(8,128)(2,1)}) custom-call(s32[1]{0:T(128)} %get-tuple-element.446.dev_ref, s32[7168]{0:T(1024)S(1)} %copy-done.1, s32[2048]{0:T(1024)S(1)} %get-tuple-element.400.lens_ref, s32[512]{0:T(512)S(1)} %copy-done.36, ...), custom_call_target="tpu_custom_call" | custom-call | tf_op jit(solution)/shard_map/cond/branch_1_fun/cond/branch_0_fun/pallas_call | solution.py:468
  125.8 1.9 collective-permute-start.13
  127.7 13.3 %collective-permute-done.10.rest_3_.rest_10_ = bf16[540,8,128]{2,1,0:T(8,128)(2,1)S(1)} collective-permute-done((bf16[540,8,128]{2,1,0:T(8,128)(2,1)}, bf16[540,8,128]{2,1,0:T(8,128)(2,1)S(1)}, u32[]{:S(2)}, u32[]{:S(2)}) %collective-permute-start.10) | collective-permute-done | bytes 1105952 | tf_op jit(solution)/shard_map/cond/branch_1_fun/cond/branch_0_fun/ppermute | solution.py:804
  144.1 6.3 %branch_0_fun.27 = (bf16[540,8,128]{2,1,0:T(8,128)(2,1)}, bf16[540,8,128]{2,1,0:T(8,128)(2,1)}, bf16[540,8,128]{2,1,0:T(8,128)(2,1)}) custom-call(s32[1]{0:T(128)} %get-tuple-element.446.dev_ref, s32[7168]{0:T(1024)S(1)} %copy-done.1, s32[2048]{0:T(1024)S(1)} %get-tuple-element.400.lens_ref, s32[512]{0:T(512)S(1)} %copy-done.36, ...), custom_call_target="tpu_custom_call" | custom-call | tf_op jit(solution)/shard_map/cond/branch_1_fun/cond/branch_0_fun/pallas_call | solution.py:468
  150.4 1.7 collective-permute-start.17
  152.1 12.7 %collective-permute-done.13.rest_13_ = bf16[540,8,128]{2,1,0:T(8,128)(2,1)S(1)} collective-permute-done((bf16[540,8,128]{2,1,0:T(8,128)(2,1)}, bf16[540,8,128]{2,1,0:T(8,128)(2,1)S(1)}, u32[]{:S(2)}, u32[]{:S(2)}) %collective-permute-start.13) | collective-permute-done | bytes 1105952 | tf_op jit(solution)/shard_map/cond/branch_1_fun/cond/branch_0_fun/ppermute | solution.py:804
  166.9 5.1 %branch_0_fun.28 = bf16[3328,8,128]{2,1,0:T(8,128)(2,1)} custom-call(s32[1]{0:T(128)} %get-tuple-element.446.dev_ref, s32[7168]{0:T(1024)S(1)} %copy-done.1, s32[2048]{0:T(1024)S(1)} %get-tuple-element.400.lens_ref, s32[512]{0:T(512)S(1)} %copy-done.36, s32[512]{0:T(512)S(1)} %get-tuple-element.409.src_ref, s32[80]{0:T(128)} %get-tuple-element.414.rest_0_, ...), custom_call_target="tpu_custom_call" | custom-call | tf_op jit(solution)/shard_map/cond/branch_1_fun/cond/branch_0_fun/pallas_call | solution.py:602
  172.0 2.5 %collective-permute-start.16 = (bf16[3328,8,128]{2,1,0:T(8,128)(2,1)}, bf16[3328,8,128]{2,1,0:T(8,128)(2,1)}, u32[]{:S(2)}, u32[]{:S(2)}) collective-permute-start(bf16[3328,8,128]{2,1,0:T(8,128)(2,1)} %branch_0_fun.28), channel_id=1, source_target_pairs={{0,1},{1,0},{2,3},{3,2},{4,5},{5,4},{6,7},{7,6},{8,9},{9,8},{10,11... | collective-permute-start | bytes 20447240 | tf_op jit(solution)/shard_map/cond/branch_1_fun/cond/branch_0_fun/ppermute | solution.py:804
  174.4 9.2 %branch_0_fun.29 = (bf16[8192,8,128]{2,1,0:T(8,128)(2,1)}, bf16[8192,8,128]{2,1,0:T(8,128)(2,1)}) custom-call(s32[1]{0:T(128)} %get-tuple-element.446.dev_ref, s32[7168]{0:T(1024)S(1)} %copy-done.1, s32[2048]{0:T(1024)S(1)} %get-tuple-element.400.lens_ref, s32[512]{0:T(512)S(1)} %copy-done.36, ...), custom_call_target="tpu_custom_call", output_to_operand_aliasing={{0}: (21, {}), {1}: (22, {})} | custom-call | tf_op jit(solution)/shard_map/cond/branch_1_fun/cond/branch_0_fun/pallas_call | solution.py:612
  183.7 4.2 %collective-permute-done.17.rest_13_ = bf16[540,8,128]{2,1,0:T(8,128)(2,1)S(1)} collective-permute-done((bf16[540,8,128]{2,1,0:T(8,128)(2,1)}, bf16[540,8,128]{2,1,0:T(8,128)(2,1)S(1)}, u32[]{:S(2)}, u32[]{:S(2)}) %collective-permute-start.17) | collective-permute-done | bytes 1105952 | tf_op jit(solution)/shard_map/cond/branch_1_fun/cond/branch_0_fun/ppermute | solution.py:804
  190.5 5.0 %branch_0_fun.30 = bf16[3328,8,128]{2,1,0:T(8,128)(2,1)} custom-call(s32[1]{0:T(128)} %get-tuple-element.446.dev_ref, s32[7168]{0:T(1024)S(1)} %copy-done.1, s32[2048]{0:T(1024)S(1)} %get-tuple-element.400.lens_ref, s32[512]{0:T(512)S(1)} %copy-done.36, s32[512]{0:T(512)S(1)} %get-tuple-element.409.src_ref, s32[80]{0:T(128)} %get-tuple-element.414.rest_0_, ...), custom_call_target="tpu_custom_call" | custom-call | tf_op jit(solution)/shard_map/cond/branch_1_fun/cond/branch_0_fun/pallas_call | solution.py:602
  195.5 2.5 %collective-permute-start.20 = (bf16[3328,8,128]{2,1,0:T(8,128)(2,1)}, bf16[3328,8,128]{2,1,0:T(8,128)(2,1)}, u32[]{:S(2)}, u32[]{:S(2)}) collective-permute-start(bf16[3328,8,128]{2,1,0:T(8,128)(2,1)} %branch_0_fun.30), channel_id=1, source_target_pairs={{0,1},{1,0},{2,3},{3,2},{4,5},{5,4},{6,7},{7,6},{8,9},{9,8},{10,11... | collective-permute-start | bytes 20447240 | tf_op jit(solution)/shard_map/cond/branch_1_fun/cond/branch_0_fun/ppermute | solution.py:804
  198.0 9.2 %branch_0_fun.31 = (bf16[8192,8,128]{2,1,0:T(8,128)(2,1)}, bf16[8192,8,128]{2,1,0:T(8,128)(2,1)}) custom-call(s32[1]{0:T(128)} %get-tuple-element.446.dev_ref, s32[7168]{0:T(1024)S(1)} %copy-done.1, s32[2048]{0:T(1024)S(1)} %get-tuple-element.400.lens_ref, s32[512]{0:T(512)S(1)} %copy-done.36, ...), custom_call_target="tpu_custom_call", output_to_operand_aliasing={{0}: (21, {}), {1}: (22, {})} | custom-call | tf_op jit(solution)/shard_map/cond/branch_1_fun/cond/branch_0_fun/pallas_call | solution.py:612
  208.9 16.9 %branch_1_fun.27 = (bf16[32,28,128]{2,1,0:T(8,128)(2,1)S(1)}, bf16[8192,8,128]{2,1,0:T(8,128)(2,1)}, bf16[8192,8,128]{2,1,0:T(8,128)(2,1)}) custom-call(s32[1]{0:T(128)} %get-tuple-element.822.dev_ref, s32[2048]{0:T(1024)S(1)} %get-tuple-element.823.lens_ref, s32[512]{0:T(512)S(1)} %get-tuple-element.824.src_ref, ...), custom_call_target="tpu_custom_call", output_to_operand_aliasing={{1}: (10, {}), {2}: (11, {})} | custom-call | tf_op jit(solution)/shard_map/cond/branch_1_fun/pallas_call | solution.py:792
  (71 shorter events, 23.1 us)
Async XLA Ops:
  10.1 6.6 %copy-start.35 = (s32[512]{0:T(512)S(1)}, s32[512]{0:T(512)}, u32[]{:S(2)}) copy-start(s32[512]{0:T(512)} %dest_ref.1) | copy-start | bytes 6148
  10.1 18.3 %copy-start.72 = (bf16[32,28,128]{2,0,1:T(8,128)(2,1)S(1)}, bf16[32,28,128]{2,0,1:T(8,128)(2,1)}, u32[]{:S(2)}) copy-start(bf16[32,28,128]{2,0,1:T(8,128)(2,1)} %param.26) | copy-start | bytes 688132
  16.6 13.2 %collective-permute-start.172 = (bf16[3456,8,128]{2,1,0:T(8,128)(2,1)}, bf16[3456,8,128]{2,1,0:T(8,128)(2,1)}, u32[]{:S(2)}, u32[]{:S(2)}) collective-permute-start(bf16[3456,8,128]{2,1,0:T(8,128)(2,1)} %get-tuple-element.857), channel_id=1, source_target_pairs={{0,1},{1,0},{2,3},{3,2},{4,5},{5,4},{6,7},{7,6},{8,9},{9,8},{10,11... | collective-permute-start | bytes 21233672 | tf_op jit(solution)/shard_map/ppermute | solution.py:804
  30.5 178.4 %copy-start.74 = (bf16[32,4,128]{2,1,0:T(4,128)(2,1)S(1)}, bf16[32,4,128]{2,1,0:T(4,128)(2,1)}, u32[]{:S(2)}) copy-start(bf16[32,4,128]{2,1,0:T(4,128)(2,1)} %get-tuple-element.836.rest_3_) | copy-start | bytes 98308 | tf_op jit(solution)/shard_map/cond
  30.5 178.4 %copy-start.76 = (bf16[32,4,128]{2,1,0:T(4,128)(2,1)S(1)}, bf16[32,4,128]{2,1,0:T(4,128)(2,1)}, u32[]{:S(2)}) copy-start(bf16[32,4,128]{2,1,0:T(4,128)(2,1)} %get-tuple-element.837.rest_4_) | copy-start | bytes 98308 | tf_op jit(solution)/shard_map/cond
  30.5 5.8 %copy-start.36 = (s32[512]{0:T(512)S(1)}, s32[512]{0:T(512)}, u32[]{:S(2)}) copy-start(s32[512]{0:T(512)} %get-tuple-element.401.dest_ref) | copy-start | bytes 6148 | tf_op jit(solution)/shard_map/cond/branch_1_fun/cond
  30.5 5.8 %copy-start.77 = (s32[32]{0:T(128)S(1)}, s32[32]{0:T(128)}, u32[]{:S(2)}) copy-start(s32[32]{0:T(128)} %get-tuple-element.407.lens_ref) | copy-start | bytes 388 | tf_op jit(solution)/shard_map/cond/branch_1_fun/cond
  36.3 9.4 %copy-start.14 = (bf16[28,32,128]{2,0,1:T(8,128)(2,1)S(1)}, bf16[28,32,128]{2,0,1:T(8,128)(2,1)}, u32[]{:S(2)}) copy-start(bf16[28,32,128]{2,0,1:T(8,128)(2,1)} %get-tuple-element.411) | copy-start | bytes 688132 | tf_op jit(solution)/shard_map/cond/branch_1_fun/cond
  36.4 15.8 %copy-start.1 = (s32[7168]{0:T(1024)S(1)}, s32[7168]{0:T(1024)}, u32[]{:S(2)}) copy-start(s32[7168]{0:T(1024)} %get-tuple-element.399.meta) | copy-start | bytes 86020 | tf_op jit(solution)/shard_map/cond/branch_1_fun/cond
  41.9 12.1 %collective-permute-start = (bf16[3456,8,128]{2,1,0:T(8,128)(2,1)}, bf16[3456,8,128]{2,1,0:T(8,128)(2,1)}, u32[]{:S(2)}, u32[]{:S(2)}) collective-permute-start(bf16[3456,8,128]{2,1,0:T(8,128)(2,1)} %branch_0_fun.20), channel_id=1, source_target_pairs={{0,1},{1,0},{2,3},{3,2},{4,5},{5,4},{6,7},{7,6},{8,9},{9,8},{10,11... | collective-permute-start | bytes 21233672 | tf_op jit(solution)/shard_map/cond/branch_1_fun/cond/branch_0_fun/ppermute | solution.py:804
  41.9 28.0 %collective-permute-start.1 = (bf16[540,8,128]{2,1,0:T(8,128)(2,1)}, bf16[540,8,128]{2,1,0:T(8,128)(2,1)S(1)}, u32[]{:S(2)}, u32[]{:S(2)}) collective-permute-start(bf16[540,8,128]{2,1,0:T(8,128)(2,1)} %get-tuple-element.405), channel_id=1, source_target_pairs={{0,2},{1,3},{2,0},{3,1},{4,6},{5,7},{6,4},{7,5},{8,10},{9,11},{10,... | collective-permute-start | bytes 3317768 | tf_op jit(solution)/shard_map/cond/branch_1_fun/cond/branch_0_fun/ppermute | solution.py:804
  44.5 27.6 %collective-permute-start.2 = (bf16[540,8,128]{2,1,0:T(8,128)(2,1)}, bf16[540,8,128]{2,1,0:T(8,128)(2,1)}, u32[]{:S(2)}, u32[]{:S(2)}) collective-permute-start(bf16[540,8,128]{2,1,0:T(8,128)(2,1)} %get-tuple-element.418), channel_id=1, source_target_pairs={{0,4},{1,5},{2,6},{3,7},{4,0},{5,1},{6,2},{7,3},{8,12},{9,13},{10,... | collective-permute-start | bytes 3317768 | tf_op jit(solution)/shard_map/cond/branch_1_fun/cond/branch_0_fun/ppermute | solution.py:804
  44.5 27.6 %collective-permute-start.3 = (bf16[540,8,128]{2,1,0:T(8,128)(2,1)}, bf16[540,8,128]{2,1,0:T(8,128)(2,1)}, u32[]{:S(2)}, u32[]{:S(2)}) collective-permute-start(bf16[540,8,128]{2,1,0:T(8,128)(2,1)} %get-tuple-element.419), channel_id=1, source_target_pairs={{0,8},{1,9},{2,10},{3,11},{4,12},{5,13},{6,14},{7,15},{8,0},{9,1},... | collective-permute-start | bytes 3317768 | tf_op jit(solution)/shard_map/cond/branch_1_fun/cond/branch_0_fun/ppermute | solution.py:804
  59.6 34.1 %collective-permute-start.4 = (bf16[540,8,128]{2,1,0:T(8,128)(2,1)}, bf16[540,8,128]{2,1,0:T(8,128)(2,1)S(1)}, u32[]{:S(2)}, u32[]{:S(2)}) collective-permute-start(bf16[540,8,128]{2,1,0:T(8,128)(2,1)} %get-tuple-element.416), channel_id=1, source_target_pairs={{0,2},{1,3},{2,0},{3,1},{4,6},{5,7},{6,4},{7,5},{8,10},{9,11},{10,... | collective-permute-start | bytes 3317768 | tf_op jit(solution)/shard_map/cond/branch_1_fun/cond/branch_0_fun/ppermute | solution.py:804
  63.4 32.3 %collective-permute-start.5 = (bf16[540,8,128]{2,1,0:T(8,128)(2,1)}, bf16[540,8,128]{2,1,0:T(8,128)(2,1)S(1)}, u32[]{:S(2)}, u32[]{:S(2)}) collective-permute-start(bf16[540,8,128]{2,1,0:T(8,128)(2,1)} %get-tuple-element.422), channel_id=1, source_target_pairs={{0,4},{1,5},{2,6},{3,7},{4,0},{5,1},{6,2},{7,3},{8,12},{9,13},{10,... | collective-permute-start | bytes 3317768 | tf_op jit(solution)/shard_map/cond/branch_1_fun/cond/branch_0_fun/ppermute | solution.py:804
  70.0 25.8 %collective-permute-start.6 = (bf16[540,8,128]{2,1,0:T(8,128)(2,1)}, bf16[540,8,128]{2,1,0:T(8,128)(2,1)}, u32[]{:S(2)}, u32[]{:S(2)}) collective-permute-start(bf16[540,8,128]{2,1,0:T(8,128)(2,1)} %get-tuple-element.423), channel_id=1, source_target_pairs={{0,8},{1,9},{2,10},{3,11},{4,12},{5,13},{6,14},{7,15},{8,0},{9,1},... | collective-permute-start | bytes 3317768 | tf_op jit(solution)/shard_map/cond/branch_1_fun/cond/branch_0_fun/ppermute | solution.py:804
  78.0 39.3 %collective-permute-start.7 = (bf16[540,8,128]{2,1,0:T(8,128)(2,1)}, bf16[540,8,128]{2,1,0:T(8,128)(2,1)S(1)}, u32[]{:S(2)}, u32[]{:S(2)}) collective-permute-start(bf16[540,8,128]{2,1,0:T(8,128)(2,1)} %get-tuple-element.420), channel_id=1, source_target_pairs={{0,2},{1,3},{2,0},{3,1},{4,6},{5,7},{6,4},{7,5},{8,10},{9,11},{10,... | collective-permute-start | bytes 3317768 | tf_op jit(solution)/shard_map/cond/branch_1_fun/cond/branch_0_fun/ppermute | solution.py:804
  79.6 39.9 %collective-permute-start.8 = (bf16[540,8,128]{2,1,0:T(8,128)(2,1)}, bf16[540,8,128]{2,1,0:T(8,128)(2,1)}, u32[]{:S(2)}, u32[]{:S(2)}) collective-permute-start(bf16[540,8,128]{2,1,0:T(8,128)(2,1)} %get-tuple-element.426), channel_id=1, source_target_pairs={{0,4},{1,5},{2,6},{3,7},{4,0},{5,1},{6,2},{7,3},{8,12},{9,13},{10,... | collective-permute-start | bytes 3317768 | tf_op jit(solution)/shard_map/cond/branch_1_fun/cond/branch_0_fun/ppermute | solution.py:804
  93.7 25.8 %collective-permute-start.9 = (bf16[540,8,128]{2,1,0:T(8,128)(2,1)}, bf16[540,8,128]{2,1,0:T(8,128)(2,1)}, u32[]{:S(2)}, u32[]{:S(2)}) collective-permute-start(bf16[540,8,128]{2,1,0:T(8,128)(2,1)} %get-tuple-element.427), channel_id=1, source_target_pairs={{0,8},{1,9},{2,10},{3,11},{4,12},{5,13},{6,14},{7,15},{8,0},{9,1},... | collective-permute-start | bytes 3317768 | tf_op jit(solution)/shard_map/cond/branch_1_fun/cond/branch_0_fun/ppermute | solution.py:804
  102.7 38.4 %collective-permute-start.10 = (bf16[540,8,128]{2,1,0:T(8,128)(2,1)}, bf16[540,8,128]{2,1,0:T(8,128)(2,1)S(1)}, u32[]{:S(2)}, u32[]{:S(2)}) collective-permute-start(bf16[540,8,128]{2,1,0:T(8,128)(2,1)} %get-tuple-element.424), channel_id=1, source_target_pairs={{0,2},{1,3},{2,0},{3,1},{4,6},{5,7},{6,4},{7,5},{8,10},{9,11},{10,... | collective-permute-start | bytes 3317768 | tf_op jit(solution)/shard_map/cond/branch_1_fun/cond/branch_0_fun/ppermute | solution.py:804
  104.4 38.7 %collective-permute-start.11 = (bf16[540,8,128]{2,1,0:T(8,128)(2,1)}, bf16[540,8,128]{2,1,0:T(8,128)(2,1)S(1)}, u32[]{:S(2)}, u32[]{:S(2)}) collective-permute-start(bf16[540,8,128]{2,1,0:T(8,128)(2,1)} %get-tuple-element.430), channel_id=1, source_target_pairs={{0,4},{1,5},{2,6},{3,7},{4,0},{5,1},{6,2},{7,3},{8,12},{9,13},{10,... | collective-permute-start | bytes 3317768 | tf_op jit(solution)/shard_map/cond/branch_1_fun/cond/branch_0_fun/ppermute | solution.py:804
  117.3 2.1 copy-start.56
  117.4 25.8 %collective-permute-start.12 = (bf16[540,8,128]{2,1,0:T(8,128)(2,1)}, bf16[540,8,128]{2,1,0:T(8,128)(2,1)}, u32[]{:S(2)}, u32[]{:S(2)}) collective-permute-start(bf16[540,8,128]{2,1,0:T(8,128)(2,1)} %get-tuple-element.431), channel_id=1, source_target_pairs={{0,8},{1,9},{2,10},{3,11},{4,12},{5,13},{6,14},{7,15},{8,0},{9,1},... | collective-permute-start | bytes 3317768 | tf_op jit(solution)/shard_map/cond/branch_1_fun/cond/branch_0_fun/ppermute | solution.py:804
  125.8 38.9 %collective-permute-start.13 = (bf16[540,8,128]{2,1,0:T(8,128)(2,1)}, bf16[540,8,128]{2,1,0:T(8,128)(2,1)S(1)}, u32[]{:S(2)}, u32[]{:S(2)}) collective-permute-start(bf16[540,8,128]{2,1,0:T(8,128)(2,1)} %get-tuple-element.428), channel_id=1, source_target_pairs={{0,2},{1,3},{2,0},{3,1},{4,6},{5,7},{6,4},{7,5},{8,10},{9,11},{10,... | collective-permute-start | bytes 3317768 | tf_op jit(solution)/shard_map/cond/branch_1_fun/cond/branch_0_fun/ppermute | solution.py:804
  127.7 39.2 %collective-permute-start.14 = (bf16[540,8,128]{2,1,0:T(8,128)(2,1)}, bf16[540,8,128]{2,1,0:T(8,128)(2,1)}, u32[]{:S(2)}, u32[]{:S(2)}) collective-permute-start(bf16[540,8,128]{2,1,0:T(8,128)(2,1)} %get-tuple-element.437), channel_id=1, source_target_pairs={{0,4},{1,5},{2,6},{3,7},{4,0},{5,1},{6,2},{7,3},{8,12},{9,13},{10,... | collective-permute-start | bytes 3317768 | tf_op jit(solution)/shard_map/cond/branch_1_fun/cond/branch_0_fun/ppermute | solution.py:804
  141.1 25.8 %collective-permute-start.15 = (bf16[540,8,128]{2,1,0:T(8,128)(2,1)}, bf16[540,8,128]{2,1,0:T(8,128)(2,1)}, u32[]{:S(2)}, u32[]{:S(2)}) collective-permute-start(bf16[540,8,128]{2,1,0:T(8,128)(2,1)} %get-tuple-element.438), channel_id=1, source_target_pairs={{0,8},{1,9},{2,10},{3,11},{4,12},{5,13},{6,14},{7,15},{8,0},{9,1},... | collective-permute-start | bytes 3317768 | tf_op jit(solution)/shard_map/cond/branch_1_fun/cond/branch_0_fun/ppermute | solution.py:804
  150.4 37.4 %collective-permute-start.17 = (bf16[540,8,128]{2,1,0:T(8,128)(2,1)}, bf16[540,8,128]{2,1,0:T(8,128)(2,1)S(1)}, u32[]{:S(2)}, u32[]{:S(2)}) collective-permute-start(bf16[540,8,128]{2,1,0:T(8,128)(2,1)} %get-tuple-element.432), channel_id=1, source_target_pairs={{0,2},{1,3},{2,0},{3,1},{4,6},{5,7},{6,4},{7,5},{8,10},{9,11},{10,... | collective-permute-start | bytes 3317768 | tf_op jit(solution)/shard_map/cond/branch_1_fun/cond/branch_0_fun/ppermute | solution.py:804
  152.1 37.2 %collective-permute-start.18 = (bf16[540,8,128]{2,1,0:T(8,128)(2,1)}, bf16[540,8,128]{2,1,0:T(8,128)(2,1)S(1)}, u32[]{:S(2)}, u32[]{:S(2)}) collective-permute-start(bf16[540,8,128]{2,1,0:T(8,128)(2,1)} %get-tuple-element.444), channel_id=1, source_target_pairs={{0,4},{1,5},{2,6},{3,7},{4,0},{5,1},{6,2},{7,3},{8,12},{9,13},{10,... | collective-permute-start | bytes 3317768 | tf_op jit(solution)/shard_map/cond/branch_1_fun/cond/branch_0_fun/ppermute | solution.py:804
  164.8 25.8 %collective-permute-start.19 = (bf16[540,8,128]{2,1,0:T(8,128)(2,1)}, bf16[540,8,128]{2,1,0:T(8,128)(2,1)}, u32[]{:S(2)}, u32[]{:S(2)}) collective-permute-start(bf16[540,8,128]{2,1,0:T(8,128)(2,1)} %get-tuple-element.445), channel_id=1, source_target_pairs={{0,8},{1,9},{2,10},{3,11},{4,12},{5,13},{6,14},{7,15},{8,0},{9,1},... | collective-permute-start | bytes 3317768 | tf_op jit(solution)/shard_map/cond/branch_1_fun/cond/branch_0_fun/ppermute | solution.py:804
  172.0 35.3 %collective-permute-start.16 = (bf16[3328,8,128]{2,1,0:T(8,128)(2,1)}, bf16[3328,8,128]{2,1,0:T(8,128)(2,1)}, u32[]{:S(2)}, u32[]{:S(2)}) collective-permute-start(bf16[3328,8,128]{2,1,0:T(8,128)(2,1)} %branch_0_fun.28), channel_id=1, source_target_pairs={{0,1},{1,0},{2,3},{3,2},{4,5},{5,4},{6,7},{7,6},{8,9},{9,8},{10,11... | collective-permute-start | bytes 20447240 | tf_op jit(solution)/shard_map/cond/branch_1_fun/cond/branch_0_fun/ppermute | solution.py:804
  187.8 2.7 %copy-start.69 = (bf16[540,8,128]{2,1,0:T(8,128)(2,1)}, bf16[540,8,128]{2,1,0:T(8,128)(2,1)S(1)}, u32[]{:S(2)}) copy-start(bf16[540,8,128]{2,1,0:T(8,128)(2,1)S(1)} %collective-permute-done.17.rest_13_) | copy-start | bytes 3317764 | tf_op jit(solution)/shard_map/cond/branch_1_fun/cond
  195.5 13.4 %collective-permute-start.20 = (bf16[3328,8,128]{2,1,0:T(8,128)(2,1)}, bf16[3328,8,128]{2,1,0:T(8,128)(2,1)}, u32[]{:S(2)}, u32[]{:S(2)}) collective-permute-start(bf16[3328,8,128]{2,1,0:T(8,128)(2,1)} %branch_0_fun.30), channel_id=1, source_target_pairs={{0,1},{1,0},{2,3},{3,2},{4,5},{5,4},{6,7},{7,6},{8,9},{9,8},{10,11... | collective-permute-start | bytes 20447240 | tf_op jit(solution)/shard_map/cond/branch_1_fun/cond/branch_0_fun/ppermute | solution.py:804
  (8 other events, 13.7 us)
